TPU v7x, 256 devices: a whole 4x4x8 slice. The times are simulated.
256 devices in a mesh: fsdp: 16 (over x_hi, y, core), cp: 16 (over x_lo, z).
Axes of the slice: x: 4 (x_hi: 2, x_lo: 2; x = x_hi * 2 + x_lo), y: 4, z: 8, core: 2. Of those that a mesh axis runs over, the one named last changes fastest.
Arguments:
- features: bfloat16 [16, 2048, 2560], P('fsdp', 'cp'), may hold values from -6 to 6
- query_rows: bfloat16 [16, 2048, 1280], P('fsdp', 'cp'), may hold values from -40 to 40, as said below
- key_rows: bfloat16 [16, 2048, 1280], P('fsdp', 'cp'), may hold values from -4 to 4
- value_rows: bfloat16 [16, 2048, 1280], P('fsdp', 'cp'), may hold values from -6 to 6
- attn_output: bfloat16 [16, 2048, 1280], P('fsdp', 'cp'), may hold values from -6 to 6
- grad_output: bfloat16 [16, 2048, 1280], P('fsdp', 'cp'), may hold values from -6 to 6
- log_sums: float32 [16, 2048, 10], P('fsdp', 'cp'), as said below
Outputs:
- d_query: bfloat16 [16, 2048, 1280], P('fsdp', 'cp')
- d_key: bfloat16 [16, 2048, 1280], P('fsdp', 'cp')
- d_value: bfloat16 [16, 2048, 1280], P('fsdp', 'cp')
- d_value_weight: float32 [2560, 1280], P('fsdp', 'cp')
Inputs may be any that keep to these rules, and one draw needn't show every extreme that they name: `query_rows`: queries of a clip, with key_rows and log_sums drawn together with them. log_sums[c, t, h] is the logarithm of the sum over all 2048 keys u of clip c of exp(128**-0.5 * q[t] . k[u]) for head h, computed from the bfloat16 queries and keys in float32.
All inputs are finite; a program needn't handle non-finite values.
Results may differ from a plain program's by a relative error of at most 0.02.
Values may be sent and summed in bfloat16 or wider, within the bound.
A program may use at most 128 MiB of HBM per device.

v0:
```python
import jax
import jax.numpy as jnp
from jax import lax
from jax.sharding import Mesh
from jax.sharding import PartitionSpec as P

CP = ("cp_0", "cp_1")


def side_by_side(arrays, axis, dim, along):
    both = jnp.concatenate(arrays, axis=along)
    whole, at, gathered = (lax.all_gather(both, axis, axis=dim, tiled=True), 0, [])
    for a in arrays:
        gathered.append(lax.slice_in_dim(whole, at, at + a.shape[along], axis=along))
        at += a.shape[along]
    return tuple(gathered)


def reduced_to_own(pieces, axes, sequence):
    inside = pieces.shape[1:]
    pieces = pieces.reshape(*(lax.axis_size(a) for a in axes), *inside)
    pieces = jnp.moveaxis(pieces, sequence, range(len(axes))).reshape(-1, *inside)
    for k in sequence:
        pieces = lax.psum_scatter(pieces, axes[k], scatter_dimension=0, tiled=True)
    return pieces[0]


def cut_along(array, dim, size):
    before, after = (array.shape[:dim], array.shape[dim + 1 :])
    return jnp.moveaxis(array.reshape(*before, size, -1, *after), dim, 0)


def summed_rows(array, axes, sequence, dim):
    size = lax.axis_size(axes)
    return reduced_to_own(cut_along(array, dim, size), axes, sequence)


def summed_on_arrival(array, axis, dim):
    pieces = cut_along(array, dim, lax.axis_size(axis))
    arrived = lax.all_to_all(pieces, axis, split_axis=0, concat_axis=0, tiled=True)
    return arrived.astype(jnp.float32).sum(axis=0)


def on_device(features, query_rows, key_rows, value_rows, attn_output, grad_output, log_sums):
    rows_here = query_rows.shape[1]
    proj_width = query_rows.shape[2]
    head_count = log_sums.shape[2]
    head_size = proj_width // head_count
    softmax_scale = head_size ** (-0.5)

    def as_heads(block):
        return block[0].reshape(block.shape[1], head_count, head_size)

    product = grad_output.astype(jnp.float32) * attn_output.astype(jnp.float32)
    row_delta = jnp.sum(product.reshape(1, rows_here, head_count, head_size), axis=3)
    own_query = as_heads(query_rows)
    own_key = as_heads(key_rows)
    own_value = as_heads(value_rows)
    own_grad = as_heads(grad_output)
    own_norm = log_sums[0].T
    own_delta = row_delta[0].T
    all_norms, all_deltas = side_by_side((log_sums, row_delta), CP, 1, 0)
    blocks = side_by_side((query_rows, key_rows, value_rows, grad_output), CP, 1, 0)
    key_heads = as_heads(blocks[1])
    value_heads = as_heads(blocks[2])
    scores = (
        jnp.einsum("qhd,khd->hqk", own_query, key_heads, preferred_element_type=jnp.float32)
        * softmax_scale
    )
    attn_prob = jnp.exp(scores - own_norm[:, :, None])
    grad_prob = jnp.einsum(
        "qhd,khd->hqk", own_grad, value_heads, preferred_element_type=jnp.float32
    )
    grad_score = (attn_prob * (grad_prob - own_delta[:, :, None])).astype(jnp.bfloat16)
    query_part = jnp.einsum(
        "hqk,khd->qhd", grad_score, key_heads, preferred_element_type=jnp.float32
    )
    query_heads = as_heads(blocks[0])
    grad_heads = as_heads(blocks[3])
    norm_block = all_norms[0].T
    delta_block = all_deltas[0].T
    scores = (
        jnp.einsum("qhd,khd->hqk", query_heads, own_key, preferred_element_type=jnp.float32)
        * softmax_scale
    )
    attn_prob = jnp.exp(scores - norm_block[:, :, None])
    grad_prob = jnp.einsum(
        "qhd,khd->hqk", grad_heads, own_value, preferred_element_type=jnp.float32
    )
    grad_score = (attn_prob * (grad_prob - delta_block[:, :, None])).astype(jnp.bfloat16)
    grad_score, prob_half = (grad_score, attn_prob.astype(jnp.bfloat16))
    key_total = jnp.einsum(
        "hqk,qhd->khd", grad_score, query_heads, preferred_element_type=jnp.float32
    )
    value_total = jnp.einsum(
        "hqk,qhd->khd", prob_half, grad_heads, preferred_element_type=jnp.float32
    )
    second = (key_total, value_total)
    key_total = second[0]
    value_total = second[1]
    d_query = (softmax_scale * query_part).astype(jnp.bfloat16).reshape(1, rows_here, proj_width)
    d_key = (softmax_scale * key_total).astype(jnp.bfloat16).reshape(1, rows_here, proj_width)
    d_value = value_total.astype(jnp.bfloat16).reshape(1, rows_here, proj_width)
    weight_term = jnp.einsum(
        "tf,tw->fw", features[0], d_value[0], preferred_element_type=jnp.float32
    )
    column_part = summed_rows(weight_term.astype(jnp.bfloat16), CP, (1, 0), 1).astype(jnp.float32)
    weight_part = summed_on_arrival(column_part.astype(jnp.bfloat16), "fsdp", 0)
    return (d_query, d_key, d_value, weight_part)


def solution(mesh):
    finer = Mesh(mesh.devices.reshape(mesh.shape["fsdp"], 2, 8), ("fsdp", "cp_0", "cp_1"))
    return jax.shard_map(
        on_device,
        mesh=finer,
        in_specs=(
            P("fsdp", CP, None),
            P("fsdp", CP, None),
            P("fsdp", CP, None),
            P("fsdp", CP, None),
            P("fsdp", CP, None),
            P("fsdp", CP, None),
            P("fsdp", CP, None),
        ),
        out_specs=(P("fsdp", CP, None), P("fsdp", CP, None), P("fsdp", CP, None), P("fsdp", CP)),
        check_vma=False,
    )
```

profile of v0, /device:TPU:19, one launch (start us, length us, event | category | flops | bytes accessed | tf_op | source)
XLA Modules:
  0.0 411.8 jit_solution(6972129710370174686)
XLA Ops:
  7.2 0.0 copy-start
  7.2 0.0 copy-start.5
  7.2 0.0 copy-start.6
  7.2 0.0 all-gather.2.cloned.1.call-start
  7.2 1.2 copy.80
  8.5 1.2 copy.77
  9.7 1.2 copy.78
  10.9 1.2 copy.79
  12.1 1.3 pad_maximum_fusion
  13.3 0.0 all-gather.2.cloned.1.call-update
  13.3 0.0 reduce-scatter.3.cloned.1.call-start
  13.4 0.0 copy-done.5
  13.4 0.2 copy.88
  13.6 0.1 convert_multiply_fusion
  13.8 0.0 copy-done.6
  13.8 31.9 %all_gather.7 = f32[2,2048,10]{1,0,2:T(2,128)S(1)} all-gather(f32[2,128,10]{1,0,2:T(2,128)S(1)} %pad_maximum_fusion.1), channel_id=1, replica_groups=mesh['fsdp'=16,'cp_0'=2,'cp_1'=8] {'cp_0','cp_1'}, dimensions={1}, use_global_device_ids=true | all-gather | bytes 174080 | tf_op jit(solution)/shard_map/all_gather | solution.py:12
  45.7 0.1 fusion.23
  45.8 0.1 copy_bitcast_fusion
  45.9 197.6 %all-gather.2.cloned.1.call-done = bf16[4,2048,1280]{1,2,0:T(8,128)(2,1)} async-done(((bf16[4,128,1280]{1,2,0:T(8,128)(2,1)}), bf16[4,2048,1280]{1,2,0:T(8,128)(2,1)}) %all-gather.2.cloned.1.call-update) | async-done | bytes 20971536 | tf_op jit(solution)/shard_map/all_gather | solution.py:12
  243.5 12.7 %fusion.22 = (bf16[1,2048,1280]{1,2,0:T(8,128)(2,1)S(1)}, bf16[1,2048,1280]{1,2,0:T(8,128)(2,1)S(1)}, bf16[1,2048,1280]{1,2,0:T(8,128)(2,1)}, bf16[1,2048,1280]{1,2,0:T(8,128)(2,1)}) fusion(bf16[4,2048,1280]{1,2,0:T(8,128)(2,1)} %all-gather.2.cloned.1.call-done), kind=kLoop, calls=%fused_computation.28 | loop fusion | bytes 41943040 | tf_op jit(solution)/shard_map/slice | solution.py:14
  256.2 0.0 copy-start.2
  256.2 0.0 copy-start.4
  256.2 1.7 fusion.25
  257.9 0.6 copy-done.2
  258.5 0.0 copy-start.3
  258.5 1.5 copy-done.4
  260.0 5.6 %fusion.15 = bf16[10,128,128]{2,1,0:T(8,128)(2,1)S(1)} fusion(bf16[2048,10,128]{0,2,1:T(8,128)(2,1)S(1)} %bitcast.70, f32[10,2048,128]{2,1,0:T(8,128)S(1)} %fusion.25, f32[10,2048]{1,0:T(8,128)S(1)} %get-tuple-element.31), kind=kOutput, calls=%fused_computation.18 | convolution fusion | flops 679116800 | bytes 16138240 | tf_op jit(solution)/shard_map/hqk,qhd->khd/dot_general | solution.py:95
  265.7 0.0 copy-done.3
  265.7 0.0 copy-done
  265.7 1.9 convolution_convert_fusion
  267.6 3.2 copy.95
  270.7 0.0 reduce-scatter.3.cloned.1.call-update
  270.7 0.2 reduce-scatter.5.cloned.1.call-start
  271.0 86.2 %reduce-scatter.3.cloned.1.call-done = bf16[2,2560,80]{1,2,0:T(8,128)(2,1)} async-done(((bf16[16,2560,80]{1,2,0:T(8,128)(2,1)}), bf16[2,2560,80]{1,2,0:T(8,128)(2,1)}) %reduce-scatter.3.cloned.1.call-update) | async-done | bytes 819216 | tf_op jit(solution)/shard_map/reduce_scatter | solution.py:24
  357.2 0.0 reduce-scatter.5.cloned.1.call-update
  357.2 8.2 %fusion.24 = f32[10,2048,128]{2,1,0:T(8,128)} fusion(bf16[2048,10,128]{0,2,1:T(8,128)(2,1)} %bitcast.65, bf16[128,10,128]{0,2,1:T(8,128)(2,1)S(1)} %bitcast.73), kind=kOutput, calls=%fused_computation.30 | convolution fusion | flops 671088640 | bytes 16056320 | tf_op jit(solution)/shard_map/qhd,khd->hqk/dot_general | solution.py:67
  365.3 11.6 %fusion.14 = bf16[10,128,128]{2,1,0:T(8,128)(2,1)S(1)} fusion(bf16[2048,10,128]{0,2,1:T(8,128)(2,1)} %bitcast.68, f32[10,2048,128]{2,1,0:T(8,128)} %copy-done.3, f32[10,2048]{1,0:T(8,128)S(1)} %get-tuple-element.30, f32[10,2048]{1,0:T(8,128)S(1)} %get-tuple-element.31, bf16[2048,10,128]{0,2,1:T(8,128)(2,1)} %bitcast.71, bf16[128,10,128]{0,2,1:T(8,128)(2,1)S(1)} %bitcast.78), kind=kOutput, calls=%fused_computation.17 | convolution fusion | flops 1355612160 | bytes 21790720 | tf_op jit(solution)/shard_map/hqk,qhd->khd/dot_general | solution.py:92
  377.0 3.3 reduce-scatter.5.cloned.1.call-done
  380.3 1.8 reshape.46
  382.1 1.0 copy.96
  383.1 7.1 %all-to-all-start = ((bf16[16,160,80]{1,2,0:T(8,128)(2,1)}), bf16[16,160,80]{1,2,0:T(8,128)(2,1)S(1)}, u32[]{:S(2)}, u32[]{:S(2)}) async-start(bf16[16,160,80]{1,2,0:T(8,128)(2,1)} %copy.96), calls=%async_computation.2 | async-start | bytes 1310720 | tf_op jit(solution)/shard_map/all_to_all | solution.py:40
  390.2 0.0 copy-start.1
  390.2 11.5 %fusion.13 = bf16[10,128,128]{2,1,0:T(8,128)(2,1)S(1)} fusion(bf16[2048,10,128]{0,2,1:T(8,128)(2,1)} %bitcast.66, f32[10,2048,128]{2,1,0:T(8,128)} %fusion.24, f32[10,128]{1,0:T(8,128)S(1)} %bitcast.81, f32[10,128]{1,0:T(8,128)S(1)} %bitcast.82, bf16[2048,10,128]{0,2,1:T(8,128)(2,1)} %bitcast.69, bf16[128,10,128]{0,2,1:T(8,128)(2,1)S(1)} %bitcast.72), kind=kOutput, calls=%fused_computation.16 | convolution fusion | flops 1355612160 | bytes 21637120 | tf_op jit(solution)/shard_map/hqk,khd->qhd/dot_general | solution.py:75
  401.7 0.9 copy.99
  402.6 0.9 copy.98
  403.5 0.9 copy.100
  404.4 0.0 all-to-all-done
  404.4 0.1 convert_reduce_fusion
  404.6 0.7 copy.101
  405.3 0.0 copy-done.1
  (4 shorter events, 0.1 us)
Async XLA Ops:
  7.2 258.5 %copy-start = (bf16[1,128,2560]{2,1,0:T(8,128)(2,1)S(1)}, bf16[1,128,2560]{2,1,0:T(8,128)(2,1)}, u32[]{:S(2)}) copy-start(bf16[1,128,2560]{2,1,0:T(8,128)(2,1)} %param.7) | copy-start | bytes 1966084
  7.2 6.2 %copy-start.5 = (bf16[1,128,1280]{2,1,0:T(8,128)(2,1)S(1)}, bf16[1,128,1280]{2,1,0:T(8,128)(2,1)}, u32[]{:S(2)}) copy-start(bf16[1,128,1280]{2,1,0:T(8,128)(2,1)} %param.11) | copy-start | bytes 983044
  7.2 6.6 %copy-start.6 = (f32[1,128,10]{1,0,2:T(1,128)S(1)}, f32[1,128,10]{1,0,2:T(1,128)}, u32[]{:S(2)}) copy-start(f32[1,128,10]{1,0,2:T(1,128)} %param.13) | copy-start | bytes 15364
  7.2 236.3 %all-gather.2.cloned.1.call-start = ((), (), s32[]{:S(2)}) async-start(), calls=%async_computation.3 | async-start | bytes 22282240 | tf_op jit(solution)/shard_map/all_gather | solution.py:12
  13.3 343.8 %reduce-scatter.3.cloned.1.call-start = ((), (), s32[]{:S(2)}) async-start(), calls=%async_computation.4 | async-start | bytes 7372800 | tf_op jit(solution)/shard_map/reduce_scatter | solution.py:24
  256.2 2.3 copy-start.2
  256.2 3.8 copy-start.4
  258.5 7.2 %copy-start.3 = (f32[10,2048,128]{2,1,0:T(8,128)}, f32[10,2048,128]{2,1,0:T(8,128)S(1)}, u32[]{:S(2)}) copy-start(f32[10,2048,128]{2,1,0:T(8,128)S(1)} %fusion.25) | copy-start | bytes 31457284
  270.7 109.5 %reduce-scatter.5.cloned.1.call-start = ((), (), s32[]{:S(2)}) async-start(), calls=%async_computation.5 | async-start | bytes 1228800 | tf_op jit(solution)/shard_map/reduce_scatter | solution.py:24
  383.1 21.3 %all-to-all-start = ((bf16[16,160,80]{1,2,0:T(8,128)(2,1)}), bf16[16,160,80]{1,2,0:T(8,128)(2,1)S(1)}, u32[]{:S(2)}, u32[]{:S(2)}) async-start(bf16[16,160,80]{1,2,0:T(8,128)(2,1)} %copy.96), calls=%async_computation.2 | async-start | bytes 1310720 | tf_op jit(solution)/shard_map/all_to_all | solution.py:40
  390.2 15.1 %copy-start.1 = (bf16[1,128,2560]{2,1,0:T(8,128)(2,1)S(1)}, bf16[1,128,2560]{2,1,0:T(8,128)(2,1)}, u32[]{:S(2)}) copy-start(bf16[1,128,2560]{2,1,0:T(8,128)(2,1)} %param.7) | copy-start | bytes 1966084
Sparse Core Ops, SparseCore 0:
  13.5 229.9 all-gather.1
  270.9 86.2 reduce-scatter.2
  359.7 20.5 reduce-scatter.4
where the time goes:
time: 414 us; the launch traced here: 412 us
  waiting for transfers between devices  287 us (69%)
  matrix products  40.5 us (10%)
  blocking collectives  31.9 us (8%)
  local copies, waits for them, and re-layouts  29.5 us (7%)
  between operations  13.9 us (3%)
  starting transfers between devices  7.37 us (2%)
    all_gather x1, waiting for transfers between devices, side_by_side(): lax.all_gather(both, axis, axis=dim, tiled=True)  198 us
    reduce_scatter x2, waiting for transfers between devices, reduced_to_own(): pieces = lax.psum_scatter(pieces, axes[k], scatter_dimension=0, tiled=True)  89.5 us
    all_gather x1, blocking collectives, side_by_side(): lax.all_gather(both, axis, axis=dim, tiled=True)  31.9 us
    slice x2, local copies, waits for them, and re-layouts, side_by_side(): lax.slice_in_dim(whole, at, at + a.shape[along], axis=along)  12.9 us
    dot_general x1, matrix products, on_device(): jnp.einsum('hqk,qhd->khd', grad_score, query_heads, preferred_element_typ...  11.6 us
    dot_general x1, matrix products, on_device(): jnp.einsum('hqk,khd->qhd', grad_score, key_heads, preferred_element_type=...  11.5 us
    unnamed x24, local copies, waits for them, and re-layouts  10.6 us
  transfers between devices with their start and end apart: 4, of which 3 were waited for; matrix products, arithmetic and copies ran while one was open for 8% of the time, Pallas kernels for 0%

commit v1 on v0

v1 whole, which is shorter than its diff:
```python
import functools

import jax
import jax.numpy as jnp
from jax import lax
from jax.experimental import pallas as pl
from jax.experimental.pallas import tpu as pltpu
from jax.sharding import Mesh
from jax.sharding import PartitionSpec as P

AXES = ("x_hi", "y", "core", "x_lo", "z")
FSDP = ("x_hi", "y", "core")
CP = ("x_lo", "z")
LOG2E = 1.4426950408889634
HEADS = 10
N_CP = 16
N_Z = 8
MESH = pl.DeviceIdType.MESH


def owner_of(head, parity):
    spare = head >= N_Z
    z = jnp.where(spare, 2 * parity + 4 * (head - N_Z), head)
    x = jnp.where(spare, 1 - parity, lax.rem(head + parity, 2))
    return x, z


def head_of(x, z, parity):
    first = x == lax.rem(z + parity, 2)
    spare = jnp.where(z == 2 * parity, N_Z, jnp.where(z == 2 * parity + 4, N_Z + 1, HEADS))
    return jnp.where(first, z, spare)


def attend_kernel(
    q_in, k_in, v_in, g_in, s_in, dq_out, dk_out, dv_out,
    q_buf, k_buf, v_buf, g_buf, s_buf, dq_acc, dk_acc, dv_acc, done, back,
    send_sem, recv_sem, ret_send, ret_recv, out_sem, *, scale, rows
):
    x, z, parity = lax.axis_index("x_lo"), lax.axis_index("z"), lax.axis_index("core")
    me = x * N_Z + z
    mine = head_of(x, z, parity)
    active = mine < HEADS
    span = 128

    barrier = pltpu.get_barrier_semaphore()

    def greet(j, _):
        peer = lax.rem(me + j, N_CP)
        pl.semaphore_signal(
            barrier, inc=1,
            device_id={"x_lo": peer // N_Z, "z": lax.rem(peer, N_Z)}, device_id_type=MESH)
        return 0

    lax.fori_loop(1, N_CP, greet, 0)
    pl.semaphore_wait(barrier, N_CP - 1)

    ins = (k_in, q_in, v_in, g_in)
    bufs = (k_buf, q_buf, v_buf, g_buf)

    def sources(head):
        cols = pl.ds(pl.multiple_of(head * span, span), span)
        return [a.at[0, :, cols] for a in ins] + [s_in.at[head]]

    def targets(block):
        return [b.at[block] for b in bufs] + [s_buf.at[block]]

    def head_at(i):
        off = jnp.where(lax.rem(i, 2) == 0, i // 2 + 1, jnp.where(i == 7, 0, N_Z - (i + 1) // 2))
        return jnp.where(i < N_Z, lax.rem(z + off, N_Z), i)

    def send(i, _):
        head = head_at(i)
        ox, oz = owner_of(head, parity)
        away = head != mine

        @pl.when(away)
        def _():
            for t, (src, dst) in enumerate(zip(sources(head), targets(me))):
                pltpu.make_async_remote_copy(
                    src_ref=src, dst_ref=dst, send_sem=send_sem.at[t, head],
                    recv_sem=recv_sem.at[t, me], device_id={"x_lo": ox, "z": oz},
                    device_id_type=MESH).start()

        @pl.when(jnp.logical_not(away))
        def _():
            for t, (src, dst) in enumerate(zip(sources(head), targets(me))):
                pltpu.make_async_copy(src, dst, recv_sem.at[t, me]).start()

        return 0

    lax.fori_loop(0, HEADS, send, 0)

    @pl.when(active)
    def _():
        def arrive(r, _):
            for t, (src, dst) in enumerate(zip(sources(0), targets(r))):
                pltpu.make_async_copy(src, dst, recv_sem.at[t, r]).wait()
            return 0

        lax.fori_loop(0, N_CP, arrive, 0)
        dk_acc[...] = jnp.zeros_like(dk_acc)
        dv_acc[...] = jnp.zeros_like(dv_acc)
        TB, UB = 4, 4

        def query_step(tb, _):
            qs = pl.ds(tb * TB, TB)
            q = q_buf[qs].reshape(TB * rows, span)
            g = g_buf[qs].reshape(TB * rows, span)
            lse = jnp.concatenate([s_buf[tb * TB + i, 0:1, :] for i in range(TB)], axis=1)
            delta = jnp.concatenate([s_buf[tb * TB + i, 1:2, :] for i in range(TB)], axis=1)

            def key_step(ub, dq):
                us = pl.ds(ub * UB, UB)
                k = k_buf[us].reshape(UB * rows, span)
                v = v_buf[us].reshape(UB * rows, span)
                nt = (((1,), (1,)), ((), ()))
                st = lax.dot_general(k, q, nt, preferred_element_type=jnp.float32)
                prob = jnp.exp2(st * (scale * LOG2E) - lse)
                dp = lax.dot_general(v, g, nt, preferred_element_type=jnp.float32)
                ds = (prob * (dp - delta)).astype(jnp.bfloat16)
                p16 = prob.astype(jnp.bfloat16)
                dv = jnp.dot(p16, g, preferred_element_type=jnp.float32)
                dk = jnp.dot(ds, q, preferred_element_type=jnp.float32)
                rs = pl.ds(pl.multiple_of(ub * UB * rows, UB * rows), UB * rows)
                dv_acc[rs, :] += dv
                dk_acc[rs, :] += dk
                return dq + lax.dot_general(
                    ds, k, (((0,), (0,)), ((), ())), preferred_element_type=jnp.float32)

            dq = lax.fori_loop(0, N_CP // UB, key_step, jnp.zeros((TB * rows, span), jnp.float32))
            dq_acc[pl.ds(pl.multiple_of(tb * TB * rows, TB * rows), TB * rows), :] = dq
            return 0

        lax.fori_loop(0, N_CP // TB, query_step, 0)
        done[0] = dv_acc[...].astype(jnp.bfloat16).reshape(N_CP, rows, span)
        done[1] = (dk_acc[...] * scale).astype(jnp.bfloat16).reshape(N_CP, rows, span)
        done[2] = (dq_acc[...] * scale).astype(jnp.bfloat16).reshape(N_CP, rows, span)

        cols = pl.ds(pl.multiple_of(mine * span, span), span)
        for t in range(3):
            def give(j, _):
                peer = lax.rem(me + j, N_CP)
                pltpu.make_async_remote_copy(
                    src_ref=done.at[t, peer], dst_ref=back.at[t, :, cols],
                    send_sem=ret_send.at[t, peer], recv_sem=ret_recv.at[t, mine],
                    device_id={"x_lo": peer // N_Z, "z": lax.rem(peer, N_Z)},
                    device_id_type=MESH).start()
                return 0

            lax.fori_loop(1, N_CP, give, 0)
            back[t, :, cols] = done[t, me]

    outs = (dv_out, dk_out, dq_out)
    for t in range(3):
        def collect(h, _):
            @pl.when(h != mine)
            def _():
                cols = pl.ds(pl.multiple_of(h * span, span), span)
                pltpu.make_async_copy(done.at[t, 0], back.at[t, :, cols], ret_recv.at[t, h]).wait()
            return 0

        lax.fori_loop(0, HEADS, collect, 0)
        pltpu.make_async_copy(back.at[t], outs[t].at[0], out_sem.at[t]).start()

    def sent(head, _):
        @pl.when(head != mine)
        def _():
            for t, (src, dst) in enumerate(zip(sources(head), targets(me))):
                pltpu.make_async_copy(src, dst, send_sem.at[t, head]).wait()
        return 0

    lax.fori_loop(0, HEADS, sent, 0)

    @pl.when(active)
    def _():
        def gave(j, _):
            peer = lax.rem(me + j, N_CP)
            for t in range(3):
                pltpu.make_async_copy(
                    done.at[t, peer], done.at[t, peer], ret_send.at[t, peer]).wait()
            return 0

        lax.fori_loop(1, N_CP, gave, 0)

    for t in range(3):
        pltpu.make_async_copy(back.at[t], outs[t].at[0], out_sem.at[t]).wait()


def attend(q, k, v, g, stats):
    _, rows, width = q.shape
    any_spec = pl.BlockSpec(memory_space=pl.ANY)
    block = pltpu.VMEM((N_CP, rows, 128), jnp.bfloat16)
    acc = pltpu.VMEM((N_CP * rows, 128), jnp.float32)
    out = jax.ShapeDtypeStruct(q.shape, jnp.bfloat16)
    return pl.pallas_call(
        functools.partial(attend_kernel, scale=128**-0.5, rows=rows),
        out_shape=(out, out, out),
        in_specs=[any_spec] * 5,
        out_specs=(any_spec,) * 3,
        scratch_shapes=[
            block, block, block, block,
            pltpu.VMEM((N_CP, 8, rows), jnp.float32),
            acc, acc, acc,
            pltpu.VMEM((3, N_CP, rows, 128), jnp.bfloat16),
            pltpu.VMEM((3, rows, width), jnp.bfloat16),
            pltpu.SemaphoreType.DMA((5, HEADS)),
            pltpu.SemaphoreType.DMA((5, N_CP)),
            pltpu.SemaphoreType.DMA((3, N_CP)),
            pltpu.SemaphoreType.DMA((3, HEADS)),
            pltpu.SemaphoreType.DMA((3,)),
        ],
        compiler_params=pltpu.CompilerParams(collective_id=0, has_side_effects=True),
        name="attend",
    )(q, k, v, g, stats)


def reduced_to_own(pieces, axes, sequence):
    inside = pieces.shape[1:]
    pieces = pieces.reshape(*(lax.axis_size(a) for a in axes), *inside)
    pieces = jnp.moveaxis(pieces, sequence, range(len(axes))).reshape(-1, *inside)
    for k in sequence:
        pieces = lax.psum_scatter(pieces, axes[k], scatter_dimension=0, tiled=True)
    return pieces[0]


def cut_along(array, dim, size):
    before, after = (array.shape[:dim], array.shape[dim + 1 :])
    return jnp.moveaxis(array.reshape(*before, size, -1, *after), dim, 0)


def on_device(features, query_rows, key_rows, value_rows, attn_output, grad_output, log_sums):
    rows = query_rows.shape[1]
    product = grad_output.astype(jnp.float32) * attn_output.astype(jnp.float32)
    delta = jnp.sum(product.reshape(rows, HEADS, 128), axis=2).T
    lse = log_sums[0].T * LOG2E
    stats = jnp.stack([lse, delta] + [jnp.zeros_like(lse)] * 6, axis=1)
    d_query, d_key, d_value = attend(query_rows, key_rows, value_rows, grad_output, stats)
    weight_term = jnp.einsum(
        "tf,tw->fw", features[0], d_value[0], preferred_element_type=jnp.float32
    )
    pieces = cut_along(weight_term.astype(jnp.bfloat16), 1, N_CP)
    column_part = reduced_to_own(pieces, CP, (1, 0))
    pieces = cut_along(column_part, 0, 16)
    arrived = lax.all_to_all(pieces, FSDP, split_axis=0, concat_axis=0, tiled=True)
    return d_query, d_key, d_value, arrived.astype(jnp.float32).sum(axis=0)


def solution(mesh):
    finer = Mesh(mesh.devices.reshape(2, 4, 2, 2, 8), AXES)
    rows = P(FSDP, CP, None)
    return jax.shard_map(
        on_device, mesh=finer, in_specs=(rows,) * 7,
        out_specs=(rows, rows, rows, P(FSDP, CP)), check_vma=False,
    )
```

time: 414 us -> 233 us (0.56)
  waiting for transfers between devices: 287 us -> 113 us
  Pallas kernels: 0 us -> 78 us
  matrix products: 40.5 us -> 2.86 us
  blocking collectives: 31.9 us -> 0 us
  local copies, waits for them, and re-layouts: 29.5 us -> 11.4 us
    all_gather x1 -> x0, waiting for transfers between devices: 198 us -> none  [side_by_side(): lax.all_gather(both, axis, axis=dim, tiled=True)]
    pallas_call x0 -> x1, Pallas kernels: none -> 78 us  [attend(): pl.pallas_call(functools.partial(attend_kernel, scale=128 ** (-0.5), rows...]
    dot_general x5 -> x0, matrix products: 38.6 us -> none  [the longest x1 11.6 us: on_device(): jnp.einsum('hqk,qhd->khd', grad_score, query_heads, preferred_element_typ...]
    all_gather x1 -> x0, blocking collectives: 31.9 us -> none  [side_by_side(): lax.all_gather(both, axis, axis=dim, tiled=True)]
    reduce_scatter x2, waiting for transfers between devices: 89.5 us -> 103 us  [reduced_to_own(): pieces = lax.psum_scatter(pieces, axes[k], scatter_dimension=0, tiled=True)]
    slice x2 -> x0, local copies, waits for them, and re-layouts: 12.9 us -> none  [side_by_side(): lax.slice_in_dim(whole, at, at + a.shape[along], axis=along)]
    all_to_all x1, waiting for transfers between devices: 0.01 us -> 10.6 us  [on_device(): lax.all_to_all(pieces, FSDP, split_axis=0, concat_axis=0, tiled=True)]
    unnamed x24 -> x14, local copies, waits for them, and re-layouts: 10.6 us -> 5.29 us
  transfers between devices with their start and end apart: 4 -> 3, of which waited for: 3 -> 3; matrix products, arithmetic and copies ran while one was open for 8% -> 0% of each run, Pallas kernels for 0% -> 0%
where the time goes in v1:
time: 233 us; the launch traced here: 228 us
  waiting for transfers between devices  113 us (48%)
  Pallas kernels  78 us (33%)
  between operations  14.1 us (6%)
  local copies, waits for them, and re-layouts  11.4 us (5%)
  starting transfers between devices  7.15 us (3%)
  matrix products  2.86 us (1%)
    reduce_scatter x2, waiting for transfers between devices, reduced_to_own(): pieces = lax.psum_scatter(pieces, axes[k], scatter_dimension=0, tiled=True)  103 us
    pallas_call x1, Pallas kernels, attend(): pl.pallas_call(functools.partial(attend_kernel, scale=128 ** (-0.5), rows...  78 us
    all_to_all x1, waiting for transfers between devices, on_device(): lax.all_to_all(pieces, FSDP, split_axis=0, concat_axis=0, tiled=True)  10.6 us
    all_to_all x1, starting transfers between devices, on_device(): lax.all_to_all(pieces, FSDP, split_axis=0, concat_axis=0, tiled=True)  7.07 us
    unnamed x14, local copies, waits for them, and re-layouts  5.29 us
  transfers between devices with their start and end apart: 3, of which 3 were waited for; matrix products, arithmetic and copies ran while one was open for 0% of the time, Pallas kernels for 0%

profile of v1, /device:TPU:19, one launch (start us, length us, event | category | flops | bytes accessed | tf_op | source)
XLA Modules:
  0.0 228.4 jit_solution(3965336187262315827)
XLA Ops:
  7.2 0.0 copy-start
  7.2 0.0 reduce-scatter.3.cloned.1.call-start
  7.2 0.1 pad.3.clone
  7.3 0.1 pad.2.clone
  7.4 0.7 fusion.2
  8.1 1.2 copy.21
  9.3 1.2 copy.20
  10.5 0.1 convert_multiply_fusion
  10.6 0.7 maximum_maximum_fusion.s_in
  11.3 78.0 %attend.1 = (bf16[1,128,1280]{2,1,0:T(8,128)(2,1)}, bf16[1,128,1280]{2,1,0:T(8,128)(2,1)}, bf16[1,128,1280]{2,1,0:T(8,128)(2,1)}) custom-call(bf16[1,128,1280]{2,1,0:T(8,128)(2,1)} %q_in.1, bf16[1,128,1280]{2,1,0:T(8,128)(2,1)} %k_in.1, bf16[1,128,1280]{2,1,0:T(8,128)(2,1)} %v_in.1, bf16[1,128,1280]{2,1,0:T(8,128)(2,1)} %g_in.1, ...), custom_call_target="tpu_custom_call" | custom-call | tf_op jit(solution)/shard_map/attend/pallas_call | solution.py:195
  89.3 0.0 copy-done
  89.3 2.9 %convolution_convert_fusion = bf16[1280,2560]{1,0:T(8,128)(2,1)S(1)} fusion(bf16[1,128,2560]{2,1,0:T(8,128)(2,1)S(1)} %copy-done, bf16[1,128,1280]{2,1,0:T(8,128)(2,1)} %get-tuple-element.20), kind=kOutput, calls=%fused_computation | convolution fusion | flops 842137600 | bytes 7536640 | tf_op jit(solution)/shard_map/tf,tw->fw/dot_general | solution.py:238
  92.2 3.2 %copy.22 = bf16[8,2,2560,80]{2,3,1,0:T(8,128)(2,1)} copy(bf16[8,2,2560,80]{2,3,0,1:T(8,128)(2,1)S(1)} %bitcast.24) | data formatting | bytes 13107200 | tf_op jit(solution)/shard_map/transpose | solution.py:220
  95.4 0.0 copy-start.3
  95.4 0.0 copy-start.2
  95.4 0.0 copy-start.1
  95.4 0.0 reduce-scatter.3.cloned.1.call-update
  95.4 0.0 reduce-scatter.5.cloned.1.call-start
  95.4 79.5 %reduce-scatter.3.cloned.1.call-done = bf16[2,2560,80]{1,2,0:T(8,128)(2,1)} async-done(((bf16[16,2560,80]{1,2,0:T(8,128)(2,1)}), bf16[2,2560,80]{1,2,0:T(8,128)(2,1)}) %reduce-scatter.3.cloned.1.call-update) | async-done | bytes 819216 | tf_op jit(solution)/shard_map/reduce_scatter | solution.py:222
  175.0 0.0 reduce-scatter.5.cloned.1.call-update
  175.0 23.1 %reduce-scatter.5.cloned.1.call-done = bf16[1,2560,80]{1,2,0:T(8,128)(2,1)} async-done(((bf16[2,2560,80]{1,2,0:T(8,128)(2,1)}), bf16[1,2560,80]{1,2,0:T(8,128)(2,1)}) %reduce-scatter.5.cloned.1.call-update) | async-done | bytes 409616 | tf_op jit(solution)/shard_map/reduce_scatter | solution.py:222
  198.1 1.8 reshape_squeeze.3
  199.9 1.0 copy.23
  200.9 7.1 %all-to-all-start = ((bf16[16,160,80]{1,2,0:T(8,128)(2,1)}), bf16[16,160,80]{1,2,0:T(8,128)(2,1)S(1)}, u32[]{:S(2)}, u32[]{:S(2)}) async-start(bf16[16,160,80]{1,2,0:T(8,128)(2,1)} %copy.23), calls=%async_computation.2 | async-start | bytes 1310720 | tf_op jit(solution)/shard_map/all_to_all | solution.py:244
  208.0 10.6 %all-to-all-done = bf16[16,160,80]{1,2,0:T(8,128)(2,1)S(1)} async-done(((bf16[16,160,80]{1,2,0:T(8,128)(2,1)}), bf16[16,160,80]{1,2,0:T(8,128)(2,1)S(1)}, u32[]{:S(2)}, u32[]{:S(2)}) %all-to-all-start) | async-done | bytes 409632 | tf_op jit(solution)/shard_map/all_to_all | solution.py:244
  218.6 0.1 convert_reduce_fusion
  218.7 0.7 copy.25
  219.4 0.0 copy-done.3
  219.4 0.7 copy.33
  220.1 0.0 copy-done.2
  220.1 0.7 copy.34
  220.9 0.0 copy-done.1
  220.9 0.7 copy.35
  (5 shorter events, 0.1 us)
Async XLA Ops:
  7.2 82.2 %copy-start = (bf16[1,128,2560]{2,1,0:T(8,128)(2,1)S(1)}, bf16[1,128,2560]{2,1,0:T(8,128)(2,1)}, u32[]{:S(2)}) copy-start(bf16[1,128,2560]{2,1,0:T(8,128)(2,1)} %param.7) | copy-start | bytes 1966084
  7.2 167.8 %reduce-scatter.3.cloned.1.call-start = ((), (), s32[]{:S(2)}) async-start(), calls=%async_computation.3 | async-start | bytes 7372800 | tf_op jit(solution)/shard_map/reduce_scatter | solution.py:222
  95.4 124.0 %copy-start.3 = (bf16[1,128,1280]{2,1,0:T(8,128)(2,1)S(1)}, bf16[1,128,1280]{2,1,0:T(8,128)(2,1)}, u32[]{:S(2)}) copy-start(bf16[1,128,1280]{2,1,0:T(8,128)(2,1)} %get-tuple-element.18) | copy-start | bytes 983044
  95.4 124.8 %copy-start.2 = (bf16[1,128,1280]{2,1,0:T(8,128)(2,1)S(1)}, bf16[1,128,1280]{2,1,0:T(8,128)(2,1)}, u32[]{:S(2)}) copy-start(bf16[1,128,1280]{2,1,0:T(8,128)(2,1)} %get-tuple-element.19) | copy-start | bytes 983044
  95.4 125.5 %copy-start.1 = (bf16[1,128,1280]{2,1,0:T(8,128)(2,1)S(1)}, bf16[1,128,1280]{2,1,0:T(8,128)(2,1)}, u32[]{:S(2)}) copy-start(bf16[1,128,1280]{2,1,0:T(8,128)(2,1)} %get-tuple-element.20) | copy-start | bytes 983044
  95.4 102.7 %reduce-scatter.5.cloned.1.call-start = ((), (), s32[]{:S(2)}) async-start(), calls=%async_computation.4 | async-start | bytes 1228800 | tf_op jit(solution)/shard_map/reduce_scatter | solution.py:222
  200.9 17.6 %all-to-all-start = ((bf16[16,160,80]{1,2,0:T(8,128)(2,1)}), bf16[16,160,80]{1,2,0:T(8,128)(2,1)S(1)}, u32[]{:S(2)}, u32[]{:S(2)}) async-start(bf16[16,160,80]{1,2,0:T(8,128)(2,1)} %copy.23), calls=%async_computation.2 | async-start | bytes 1310720 | tf_op jit(solution)/shard_map/all_to_all | solution.py:244
Sparse Core Ops, SparseCore 0:
  95.5 79.4 reduce-scatter.2
  177.5 20.5 reduce-scatter.4

commit v2 on v1

v2 whole, which is shorter than its diff:
```python
import functools

import jax
import jax.numpy as jnp
from jax import lax
from jax.experimental import pallas as pl
from jax.experimental.pallas import tpu as pltpu
from jax.sharding import Mesh
from jax.sharding import PartitionSpec as P

AXES = ("x_hi", "y", "core", "x_lo", "z")
FSDP = ("x_hi", "y", "core")
CP = ("x_lo", "z")
LOG2E = 1.4426950408889634
HEADS = 10
SPAN = 128
N_CP = 16
N_Z = 8
MESH = pl.DeviceIdType.MESH
F32 = jnp.float32
BF16 = jnp.bfloat16
NT = (((1,), (1,)), ((), ()))
TN = (((0,), (0,)), ((), ()))


def owner_of(head, parity):
    spare = head >= N_Z
    z = jnp.where(spare, 2 * parity + 4 * (head - N_Z), head)
    x = jnp.where(spare, 1 - parity, lax.rem(head + parity, 2))
    return x, z


def head_of(x, z, parity):
    first = x == lax.rem(z + parity, 2)
    spare = jnp.where(z == 2 * parity, N_Z, jnp.where(z == 2 * parity + 4, N_Z + 1, HEADS))
    return jnp.where(first, z, spare)


def step_kernel(
    f_in, q_in, k_in, v_in, o_in, g_in, l_in, dq_out, dk_out, dv_out, dw_out,
    q_buf, k_buf, v_buf, g_buf, s_buf, prob, dq_acc, done, back,
    g_own, o_own, l_own, s_own, f_own, ft_own, ft_buf, dv_buf,
    half_send, half_recv, part, x_send, x_recv, z_send, z_recv, total,
    in_sem, send_sem, recv_sem, ret_send, ret_recv, out_sem,
    f_ssem, f_rsem, y_ssem, y_rsem, d_ssem, d_rsem, x_ssem, x_rsem, z_ssem, z_rsem,
    *, scale, rows
):
    xh, y, core = lax.axis_index("x_hi"), lax.axis_index("y"), lax.axis_index("core")
    xl, z = lax.axis_index("x_lo"), lax.axis_index("z")
    x = 2 * xh + xl
    me = xl * N_Z + z
    mine = head_of(xl, z, core)
    active = mine < HEADS
    feat = f_in.shape[2]
    half_f, quarter_f = feat // 2, feat // 4
    half_w = q_in.shape[2] // 2
    blk = quarter_f // 4
    col = half_w // N_Z

    def cp_id(peer):
        return {"x_lo": peer // N_Z, "z": lax.rem(peer, N_Z)}

    def x_id(p):
        return {"x_hi": p // 2, "x_lo": lax.rem(p, 2)}

    to_xh, to_xl, to_y, to_core = y // 2, lax.rem(y, 2), 2 * core + xh, xl
    from_y, from_core, from_xh, from_xl = 2 * xh + xl, y // 2, lax.rem(y, 2), core
    loop = jnp.logical_and(
        jnp.logical_and(to_xh == xh, to_xl == xl), jnp.logical_and(to_y == y, to_core == core))

    def to_id(zz):
        return {"x_hi": to_xh, "y": to_y, "core": to_core, "x_lo": to_xl, "z": zz}

    loads = [
        pltpu.make_async_copy(g_in.at[0], g_own, in_sem.at[0]),
        pltpu.make_async_copy(o_in.at[0], o_own, in_sem.at[1]),
        pltpu.make_async_copy(l_in.at[0], l_own, in_sem.at[2]),
        pltpu.make_async_copy(f_in.at[0], f_own, in_sem.at[3]),
    ]
    for c in loads:
        c.start()

    barrier = pltpu.get_barrier_semaphore()

    def signal(where):
        pl.semaphore_signal(barrier, inc=1, device_id=where, device_id_type=MESH)

    def greet_cp(j, _):
        signal(cp_id(lax.rem(me + j, N_CP)))
        return 0

    def greet_quad(j, _):
        signal({"y": lax.rem(y + j, 4)})
        signal(x_id(lax.rem(x + j, 4)))
        return 0

    def greet_from(zz, _):
        @pl.when(jnp.logical_not(jnp.logical_and(loop, zz == z)))
        def _():
            signal({"x_hi": from_xh, "y": from_y, "core": from_core, "x_lo": from_xl, "z": zz})
        return 0

    lax.fori_loop(0, N_Z, greet_from, 0)
    lax.fori_loop(1, N_CP, greet_cp, 0)
    lax.fori_loop(1, 4, greet_quad, 0)
    signal({"core": 1 - core})
    pl.semaphore_wait(barrier, jnp.where(loop, 29, 30))

    def head_at(i):
        off = jnp.where(lax.rem(i, 2) == 0, i // 2 + 1, jnp.where(i == 7, 0, N_Z - (i + 1) // 2))
        return jnp.where(i < N_Z, lax.rem(z + off, N_Z), i)

    def cols_of(head):
        return pl.ds(pl.multiple_of(head * SPAN, SPAN), SPAN)

    ins = (k_in, q_in, g_in, v_in)
    bufs = (k_buf, q_buf, g_buf, v_buf)

    def source(t, head):
        return ins[t].at[0, :, cols_of(head)] if t < 4 else s_own.at[head]

    def target(t, block):
        return bufs[t].at[block] if t < 4 else s_buf.at[block]

    def send_all(kinds):
        def send(i, _):
            head = head_at(i)
            ox, oz = owner_of(head, core)

            @pl.when(head != mine)
            def _():
                for t in kinds:
                    pltpu.make_async_remote_copy(
                        src_ref=source(t, head), dst_ref=target(t, me),
                        send_sem=send_sem.at[t, head], recv_sem=recv_sem.at[t, me],
                        device_id={"x_lo": ox, "z": oz}, device_id_type=MESH).start()

            @pl.when(head == mine)
            def _():
                for t in kinds:
                    if t < 4:
                        pltpu.make_async_copy(source(t, head), target(t, me), recv_sem.at[t, me]).start()
                    else:
                        s_buf[me] = s_own[head]

            return 0

        lax.fori_loop(0, HEADS, send, 0)

    send_all((0, 1, 2))

    for c in loads[:3]:
        c.wait()
    lse = jnp.concatenate([l_own[...] * LOG2E, jnp.zeros((rows, SPAN - HEADS), F32)], axis=1).T
    s_own[...] = jnp.zeros_like(s_own)
    for h in range(HEADS):
        hs = slice(h * SPAN, (h + 1) * SPAN)
        product = g_own[:, hs].astype(F32) * o_own[:, hs].astype(F32)
        s_own[h, 0:1, :] = lse[h : h + 1]
        s_own[h, 1:2, :] = jnp.sum(product.T, axis=0, keepdims=True)
    send_all((4, 3))

    loads[3].wait()

    def turn(i, _):
        at = pl.multiple_of(i * SPAN, SPAN)
        ft_own[pl.ds(at, SPAN), :] = f_own[:, pl.ds(at, SPAN)].T
        return 0

    lax.fori_loop(0, feat // SPAN, turn, 0)
    my_rows = pl.ds(pl.multiple_of(y * SPAN, SPAN), SPAN)

    def feature_copy(j):
        to = lax.rem(y + j, 4)
        start = pl.multiple_of((to // 2) * half_f, half_f)
        return pltpu.make_async_remote_copy(
            src_ref=ft_own.at[pl.ds(start, half_f), :], dst_ref=ft_buf.at[:, my_rows],
            send_sem=f_ssem.at[j], recv_sem=f_rsem.at[j], device_id={"y": to},
            device_id_type=MESH)

    for j in range(1, 4):
        feature_copy(j).start()
    ft_buf[:, my_rows] = ft_own[pl.ds(pl.multiple_of((y // 2) * half_f, half_f), half_f), :]

    @pl.when(active)
    def _():
        def arrive(kinds):
            def one(r, _):
                for t in kinds:
                    if t < 4:
                        pltpu.make_async_copy(source(t, 0), target(t, r), recv_sem.at[t, r]).wait()
                    else:
                        @pl.when(r != me)
                        def _():
                            pltpu.make_async_copy(source(t, 0), target(t, r), recv_sem.at[t, r]).wait()
                return 0
            lax.fori_loop(0, N_CP, one, 0)

        arrive((0, 1, 2, 4))
        UB = 2
        seq = N_CP * rows
        q = q_buf[...].reshape(seq, SPAN)
        g = g_buf[...].reshape(seq, SPAN)
        lse = jnp.concatenate([s_buf[i, 0:1, :] for i in range(N_CP)], axis=1)
        delta = jnp.concatenate([s_buf[i, 1:2, :] for i in range(N_CP)], axis=1)

        def value_step(ub, _):
            us = pl.ds(ub * UB, UB)
            k = k_buf[us].reshape(UB * rows, SPAN)
            st = lax.dot_general(k, q_buf[...].reshape(seq, SPAN), NT, preferred_element_type=F32)
            p = jnp.exp2(st * (scale * LOG2E) - lse)
            prob[pl.ds(pl.multiple_of(ub * UB * rows, UB * rows), UB * rows), :] = p
            dv = jnp.dot(p.astype(BF16), g_buf[...].reshape(seq, SPAN), preferred_element_type=F32)
            done[0, us] = dv.astype(BF16).reshape(UB, rows, SPAN)
            return 0

        lax.fori_loop(0, N_CP // UB, value_step, 0)

        def give_all(t):
            def give(j, _):
                peer = lax.rem(me + j, N_CP)
                pltpu.make_async_remote_copy(
                    src_ref=done.at[t, peer], dst_ref=back.at[t, :, cols_of(mine)],
                    send_sem=ret_send.at[t, peer], recv_sem=ret_recv.at[t, mine],
                    device_id=cp_id(peer), device_id_type=MESH).start()
                return 0

            lax.fori_loop(1, N_CP, give, 0)
            back[t, :, cols_of(mine)] = done[t, me]

        give_all(0)
        arrive((3,))
        dq_acc[...] = jnp.zeros_like(dq_acc)

        def key_step(ub, _):
            us = pl.ds(ub * UB, UB)
            k = k_buf[us].reshape(UB * rows, SPAN)
            v = v_buf[us].reshape(UB * rows, SPAN)
            p = prob[pl.ds(pl.multiple_of(ub * UB * rows, UB * rows), UB * rows), :]
            dp = lax.dot_general(v, g_buf[...].reshape(seq, SPAN), NT, preferred_element_type=F32)
            ds = (p * (dp - delta)).astype(BF16)
            dk = jnp.dot(ds, q_buf[...].reshape(seq, SPAN), preferred_element_type=F32)
            done[1, us] = (dk * scale).astype(BF16).reshape(UB, rows, SPAN)
            dq_acc[...] += lax.dot_general(ds, k, TN, preferred_element_type=F32)
            return 0

        lax.fori_loop(0, N_CP // UB, key_step, 0)
        give_all(1)
        done[2] = (dq_acc[...] * scale).astype(BF16).reshape(N_CP, rows, SPAN)
        give_all(2)

    outs = (dv_out, dk_out, dq_out)

    def collect_all(t):
        def collect(h, _):
            @pl.when(h != mine)
            def _():
                pltpu.make_async_copy(done.at[t, 0], back.at[t, :, cols_of(h)], ret_recv.at[t, h]).wait()
            return 0

        lax.fori_loop(0, HEADS, collect, 0)
        pltpu.make_async_copy(back.at[t], outs[t].at[0], out_sem.at[t]).start()

    collect_all(0)

    def value_copy(j):
        to = lax.rem(y + j, 4)
        cols = pl.ds(pl.multiple_of(lax.rem(to, 2) * half_w, half_w), half_w)
        return pltpu.make_async_remote_copy(
            src_ref=back.at[0, :, cols], dst_ref=dv_buf.at[my_rows, :],
            send_sem=y_ssem.at[j], recv_sem=y_rsem.at[j], device_id={"y": to},
            device_id_type=MESH)

    for j in range(1, 4):
        value_copy(j).start()
    dv_buf[my_rows, :] = back[0, :, pl.ds(pl.multiple_of(lax.rem(y, 2) * half_w, half_w), half_w)]
    for j in range(1, 4):
        feature_copy(j).wait()
    for j in range(1, 4):
        value_copy(j).wait()

    def part_of(which, p):
        at = pl.multiple_of(which * quarter_f + p * blk, blk)
        return jnp.dot(ft_buf[pl.ds(at, blk), :], dv_buf[...], preferred_element_type=F32)

    def half_copy(p):
        return pltpu.make_async_remote_copy(
            src_ref=half_send.at[p], dst_ref=half_recv.at[p], send_sem=d_ssem.at[p],
            recv_sem=d_rsem.at[p], device_id={"core": 1 - core}, device_id_type=MESH)

    def x_copy(j):
        to = lax.rem(x + j, 4)
        return pltpu.make_async_remote_copy(
            src_ref=x_send.at[j], dst_ref=x_recv.at[j], send_sem=x_ssem.at[j],
            recv_sem=x_rsem.at[j], device_id=x_id(to), device_id_type=MESH)

    order = (1, 2, 3, 0)
    for j in order:
        p = lax.rem(x + j, 4)
        half_send[p] = part_of(1 - core, p).astype(BF16)
        half_copy(p).start()
    for j in order:
        p = lax.rem(x + j, 4)
        part[...] = part_of(core, p)
        half_copy(p).wait_recv()
        both = part[...] + half_recv[p].astype(F32)
        if j:
            x_send[j] = both.astype(BF16)
            x_copy(j).start()
        else:
            part[...] = both
    both = part[...]
    for j in range(1, 4):
        x_copy(j).wait_recv()
        both += x_recv[j].astype(F32)

    gap = jnp.zeros((blk, SPAN - col), BF16)
    for zz in range(N_Z):
        piece = both[:, zz * col : (zz + 1) * col].astype(BF16)
        z_send[zz] = jnp.concatenate([piece, gap], axis=1)

    def z_copy(zz):
        return pltpu.make_async_remote_copy(
            src_ref=z_send.at[zz], dst_ref=z_recv.at[z], send_sem=z_ssem.at[zz],
            recv_sem=z_rsem.at[z], device_id=to_id(zz), device_id_type=MESH)

    def is_loop(zz):
        return jnp.logical_and(loop, zz == z)

    def z_start(i, _):
        zz = lax.rem(z + i, N_Z)

        @pl.when(jnp.logical_not(is_loop(zz)))
        def _():
            z_copy(zz).start()

        @pl.when(is_loop(zz))
        def _():
            z_recv[zz] = z_send[zz]

        return 0

    lax.fori_loop(0, N_Z, z_start, 0)
    collect_all(1)
    collect_all(2)
    total[...] = jnp.zeros_like(total)

    def z_take(zz, _):
        @pl.when(jnp.logical_not(is_loop(zz)))
        def _():
            pltpu.make_async_copy(z_send.at[zz], z_recv.at[zz], z_rsem.at[zz]).wait()

        total[...] += z_recv[zz][:, :col].astype(F32)
        return 0

    lax.fori_loop(0, N_Z, z_take, 0)
    last = pltpu.make_async_copy(total, dw_out, out_sem.at[3])
    last.start()

    def sent(head, _):
        @pl.when(head != mine)
        def _():
            for t in range(5):
                pltpu.make_async_copy(source(t, head), target(t, me), send_sem.at[t, head]).wait()
        return 0

    lax.fori_loop(0, HEADS, sent, 0)

    @pl.when(active)
    def _():
        def gave(j, _):
            peer = lax.rem(me + j, N_CP)
            for t in range(3):
                pltpu.make_async_copy(
                    done.at[t, peer], back.at[t, :, cols_of(mine)], ret_send.at[t, peer]).wait()
            return 0

        lax.fori_loop(1, N_CP, gave, 0)

    for p in range(4):
        half_copy(p).wait_send()
    for j in range(1, 4):
        x_copy(j).wait_send()

    def z_sent(zz, _):
        @pl.when(jnp.logical_not(is_loop(zz)))
        def _():
            z_copy(zz).wait_send()
        return 0

    lax.fori_loop(0, N_Z, z_sent, 0)
    for t in range(3):
        pltpu.make_async_copy(back.at[t], outs[t].at[0], out_sem.at[t]).wait()
    last.wait()


def on_device(features, query_rows, key_rows, value_rows, attn_output, grad_output, log_sums):
    _, rows, width = query_rows.shape
    feat = features.shape[2]
    seq = N_CP * rows
    blk, half_w = feat // 16, width // 2
    any_spec = pl.BlockSpec(memory_space=pl.ANY)
    block = pltpu.VMEM((N_CP, rows, SPAN), BF16)
    out = jax.ShapeDtypeStruct(query_rows.shape, BF16)
    dma = pltpu.SemaphoreType.DMA
    return pl.pallas_call(
        functools.partial(step_kernel, scale=SPAN**-0.5, rows=rows),
        out_shape=(out, out, out, jax.ShapeDtypeStruct((blk, half_w // N_Z), F32)),
        in_specs=[any_spec] * 7,
        out_specs=(any_spec,) * 4,
        scratch_shapes=[
            block, block, block, block,
            pltpu.VMEM((N_CP, 8, rows), F32),
            pltpu.VMEM((seq, seq), F32),
            pltpu.VMEM((seq, SPAN), F32),
            pltpu.VMEM((3, N_CP, rows, SPAN), BF16),
            pltpu.VMEM((3, rows, width), BF16),
            pltpu.VMEM((rows, width), BF16),
            pltpu.VMEM((rows, width), BF16),
            pltpu.VMEM((rows, HEADS), F32),
            pltpu.VMEM((HEADS, 8, rows), F32),
            pltpu.VMEM((rows, feat), BF16),
            pltpu.VMEM((feat, rows), BF16),
            pltpu.VMEM((feat // 2, 4 * rows), BF16),
            pltpu.VMEM((4 * rows, half_w), BF16),
            pltpu.VMEM((4, blk, half_w), BF16),
            pltpu.VMEM((4, blk, half_w), BF16),
            pltpu.VMEM((blk, half_w), F32),
            pltpu.VMEM((4, blk, half_w), BF16),
            pltpu.VMEM((4, blk, half_w), BF16),
            pltpu.VMEM((N_Z, blk, SPAN), BF16),
            pltpu.VMEM((N_Z, blk, SPAN), BF16),
            pltpu.VMEM((blk, half_w // N_Z), F32),
            dma((4,)),
            dma((5, HEADS)), dma((5, N_CP)), dma((3, N_CP)), dma((3, HEADS)), dma((4,)),
            dma((4,)), dma((4,)), dma((4,)), dma((4,)), dma((4,)), dma((4,)),
            dma((4,)), dma((4,)), dma((N_Z,)), dma((N_Z,)),
        ],
        compiler_params=pltpu.CompilerParams(
            collective_id=0, has_side_effects=True, vmem_limit_bytes=60 * 2**20),
        name="step",
    )(features, query_rows, key_rows, value_rows, attn_output, grad_output, log_sums)


def solution(mesh):
    finer = Mesh(mesh.devices.reshape(2, 4, 2, 2, 8), AXES)
    rows = P(FSDP, CP, None)
    return jax.shard_map(
        on_device, mesh=finer, in_specs=(rows,) * 7,
        out_specs=(rows, rows, rows, P(FSDP, CP)), check_vma=False,
    )
```

time: 233 us -> 109 us (0.47)
  the two profiles are of different devices: /device:TPU:19 before, /device:TPU:4 now
where the time goes in v2:
time: 109 us
  Pallas kernels  103 us (94%)
  local copies, waits for them, and re-layouts  5.85 us (5%)
    pallas_call x1, Pallas kernels, on_device(): pl.pallas_call(functools.partial(step_kernel, scale=SPAN ** (-0.5), rows=...  103 us
    unnamed x11, local copies, waits for them, and re-layouts  5.85 us

profile of v2, /device:TPU:4, one launch (start us, length us, event | category | flops | bytes accessed | tf_op | source)
XLA Modules:
  0.0 109.1 jit_solution(1267627437743794270)
XLA Ops:
  0.6 1.4 %copy.11.l_in = f32[1,128,10]{2,1,0:T(8,128)} copy(f32[1,128,10]{1,0,2:T(1,128)} %param.13) | data formatting | bytes 10240 | tf_op args[6]
  2.1 102.6 %step.1 = (bf16[1,128,1280]{2,1,0:T(8,128)(2,1)}, bf16[1,128,1280]{2,1,0:T(8,128)(2,1)}, bf16[1,128,1280]{2,1,0:T(8,128)(2,1)}, f32[160,80]{1,0:T(8,128)}) custom-call(bf16[1,128,2560]{2,1,0:T(8,128)(2,1)} %f_in.1, bf16[1,128,1280]{2,1,0:T(8,128)(2,1)} %q_in.1, bf16[1,128,1280]{2,1,0:T(8,128)(2,1)} %k_in.1, bf16[1,128,1280]{2,1,0:T(8,128)(2,1)} %v_in.1, ...), custom_call_target="tpu_custom_call" | custom-call | tf_op jit(solution)/shard_map/step/pallas_call | solution.py:406
  104.7 0.0 copy-start.1
  104.7 1.8 %copy.16 = bf16[1,128,1280]{2,1,0:T(8,128)(2,1)} copy(bf16[1,128,1280]{2,1,0:T(8,128)(2,1)} %get-tuple-element.8) | data formatting | bytes 655360
  106.5 0.0 copy-done.1
  106.5 0.0 copy-start
  106.5 0.7 copy.17
  107.2 0.4 copy-done
  107.6 0.0 copy-start.2
  107.6 0.7 copy.18
  108.3 0.2 copy-done.2
  108.5 0.6 copy.19
Async XLA Ops:
  104.7 1.8 %copy-start.1 = (bf16[1,128,1280]{2,1,0:T(8,128)(2,1)S(1)}, bf16[1,128,1280]{2,1,0:T(8,128)(2,1)}, u32[]{:S(2)}) copy-start(bf16[1,128,1280]{2,1,0:T(8,128)(2,1)} %get-tuple-element.9) | copy-start | bytes 983044
  106.5 1.1 copy-start
  107.6 0.9 copy-start.2

commit v3 on v2

v3 whole, which is shorter than its diff:
```python
import functools

import jax
import jax.numpy as jnp
from jax import lax
from jax.experimental import pallas as pl
from jax.experimental.pallas import tpu as pltpu
from jax.sharding import Mesh
from jax.sharding import PartitionSpec as P

AXES = ("x_hi", "y", "core", "x_lo", "z")
FSDP = ("x_hi", "y", "core")
CP = ("x_lo", "z")
LOG2E = 1.4426950408889634
HEADS = 10
SPAN = 128
N_CP = 16
N_Z = 8
MESH = pl.DeviceIdType.MESH
F32 = jnp.float32
BF16 = jnp.bfloat16
NT = (((1,), (1,)), ((), ()))
TN = (((0,), (0,)), ((), ()))


def owner_of(head, parity):
    spare = head >= N_Z
    z = jnp.where(spare, 2 * parity + 4 * (head - N_Z), head)
    x = jnp.where(spare, 1 - parity, lax.rem(head + parity, 2))
    return x, z


def head_of(x, z, parity):
    first = x == lax.rem(z + parity, 2)
    spare = jnp.where(z == 2 * parity, N_Z, jnp.where(z == 2 * parity + 4, N_Z + 1, HEADS))
    return jnp.where(first, z, spare)


def step_kernel(
    f_in, q_in, k_in, v_in, o_in, g_in, l_in, dq_out, dk_out, dv_out, dw_out,
    q_buf, k_buf, v_buf, g_buf, s_buf, prob, dq_acc, done, back,
    g_own, o_own, l_own, s_own, f_own, ft_own, ft_buf, dv_buf,
    half_send, half_recv, part, x_send, x_recv, z_send, z_recv, total,
    in_sem, send_sem, recv_sem, ret_send, ret_recv, out_sem,
    f_ssem, f_rsem, y_ssem, y_rsem, d_ssem, d_rsem, x_ssem, x_rsem, z_ssem, z_rsem,
    *, scale, rows
):
    xh, y, core = lax.axis_index("x_hi"), lax.axis_index("y"), lax.axis_index("core")
    xl, z = lax.axis_index("x_lo"), lax.axis_index("z")
    x = 2 * xh + xl
    me = 2 * z + xl
    mine = head_of(xl, z, core)
    active = mine < HEADS
    feat = f_in.shape[2]
    half_w = q_in.shape[2] // 2
    blk = feat // 16
    per = feat // 4 // SPAN
    col = half_w // N_Z

    def cp_id(peer):
        return {"x_lo": lax.rem(peer, 2), "z": peer // 2}

    y1, y0 = y // 2, lax.rem(y, 2)
    stays = y0 == xl

    def row_id(p):
        return {"x_hi": p // 2, "x_lo": lax.rem(p, 2)}

    def owner_id(zz):
        return {"x_lo": y0, "y": 2 * y1 + xl, "z": zz}

    loads = [
        pltpu.make_async_copy(g_in.at[0], g_own, in_sem.at[0]),
        pltpu.make_async_copy(o_in.at[0], o_own, in_sem.at[1]),
        pltpu.make_async_copy(l_in, l_own, in_sem.at[2]),
        pltpu.make_async_copy(f_in.at[0], f_own, in_sem.at[3]),
    ]
    for c in loads:
        c.start()

    barrier = pltpu.get_barrier_semaphore()

    def signal(where):
        pl.semaphore_signal(barrier, inc=1, device_id=where, device_id_type=MESH)

    def greet_cp(j, _):
        signal(cp_id(lax.rem(me + j, N_CP)))
        return 0

    def greet_quad(j, _):
        signal({"y": lax.rem(y + j, 4)})
        signal(row_id(lax.rem(x + j, 4)))
        return 0

    def greet_owner(zz, _):
        signal(owner_id(zz))
        return 0

    @pl.when(jnp.logical_not(stays))
    def _():
        lax.fori_loop(0, N_Z, greet_owner, 0)

    lax.fori_loop(1, N_CP, greet_cp, 0)
    lax.fori_loop(1, 4, greet_quad, 0)
    signal({"core": 1 - core})
    pl.semaphore_wait(barrier, jnp.where(stays, 22, 30))

    def far_first(i):
        return jnp.where(lax.rem(i, 2) == 0, 4 + i // 2, 3 - i // 2) % N_Z

    def head_at(i):
        return jnp.where(i < 2, N_Z + i, lax.rem(z + far_first(i - 2), N_Z))

    def cols_of(head):
        return pl.ds(pl.multiple_of(head * SPAN, SPAN), SPAN)

    ins = (k_in, q_in, g_in, v_in)
    bufs = (k_buf, q_buf, g_buf, v_buf)

    def source(t, head):
        return ins[t].at[0, :, cols_of(head)] if t < 4 else s_own.at[head]

    def target(t, block):
        return bufs[t].at[block] if t < 4 else s_buf.at[block]

    def send_all(kinds):
        def send(i, _):
            head = head_at(i)
            ox, oz = owner_of(head, core)

            @pl.when(head != mine)
            def _():
                for t in kinds:
                    pltpu.make_async_remote_copy(
                        src_ref=source(t, head), dst_ref=target(t, me),
                        send_sem=send_sem.at[t, head], recv_sem=recv_sem.at[t, me],
                        device_id={"x_lo": ox, "z": oz}, device_id_type=MESH).start()

            @pl.when(head == mine)
            def _():
                for t in kinds:
                    if t < 4:
                        pltpu.make_async_copy(source(t, head), target(t, me), recv_sem.at[t, me]).start()
                    else:
                        s_buf[me] = s_own[head]

            return 0

        lax.fori_loop(0, HEADS, send, 0)

    send_all((1, 2))

    for c in loads[:3]:
        c.wait()
    lse = l_own[...] * LOG2E
    s_own[...] = jnp.zeros_like(s_own)
    for h in range(HEADS):
        hs = slice(h * SPAN, (h + 1) * SPAN)
        product = g_own[:, hs].astype(F32) * o_own[:, hs].astype(F32)
        s_own[h, 0:1, :] = lse[h]
        s_own[h, 1:2, :] = jnp.sum(product.T, axis=0, keepdims=True)
    send_all((4,))
    send_all((0,))
    send_all((3,))

    loads[3].wait()

    def turn(i, _):
        at = pl.multiple_of(i * SPAN, SPAN)
        group = i // per
        rs = pl.ds(pl.multiple_of(lax.rem(i, per) * SPAN, SPAN), SPAN)
        ft_own[group // 2, lax.rem(group, 2), rs, :] = f_own[:, pl.ds(at, SPAN)].T
        return 0

    lax.fori_loop(0, feat // SPAN, turn, 0)
    my_rows = pl.ds(pl.multiple_of(y * SPAN, SPAN), SPAN)

    def feature_copy(j):
        to = lax.rem(y + j, 4)
        return pltpu.make_async_remote_copy(
            src_ref=ft_own.at[:, to // 2], dst_ref=ft_buf.at[:, :, my_rows],
            send_sem=f_ssem.at[j], recv_sem=f_rsem.at[j], device_id={"y": to},
            device_id_type=MESH)

    for j in range(1, 4):
        feature_copy(j).start()
    ft_buf[:, :, my_rows] = ft_own[:, y1]

    half_h = HEADS // 2

    def value_copy(h, o):
        to = h // half_h + 2 * o
        at = lax.rem(h, half_h)
        return to, pltpu.make_async_remote_copy(
            src_ref=back.at[0, :, cols_of(h)], dst_ref=dv_buf.at[my_rows, cols_of(at)],
            send_sem=y_ssem.at[h, o], recv_sem=y_rsem.at[y, at], device_id={"y": to},
            device_id_type=MESH)

    def pass_on(i, _):
        h = jnp.where(i < N_Z, lax.rem(z + far_first(i), N_Z), i)

        @pl.when(h != mine)
        def _():
            pltpu.make_async_copy(done.at[0, 0], back.at[0, :, cols_of(h)], ret_recv.at[0, h]).wait()

        for o in range(2):
            to, copy = value_copy(h, o)

            @pl.when(to != y)
            def _():
                copy.start()
        return 0

    UB = 2
    seq = N_CP * rows

    def block_at(i):
        return lax.rem(z + N_Z - far_first(i), N_Z)

    def arrive_pair(t, b):
        for xx in range(2):
            r = 2 * b + xx
            pltpu.make_async_copy(source(t, 0), target(t, r), recv_sem.at[t, r]).wait()

    def give(t, r):
        @pl.when(r != me)
        def _():
            pltpu.make_async_remote_copy(
                src_ref=done.at[t, r], dst_ref=back.at[t, :, cols_of(mine)],
                send_sem=ret_send.at[t, r], recv_sem=ret_recv.at[t, mine],
                device_id=cp_id(r), device_id_type=MESH).start()

        @pl.when(r == me)
        def _():
            back[t, :, cols_of(mine)] = done[t, me]

    @pl.when(active)
    def _():
        def arrive(kinds):
            def one(r, _):
                for t in kinds:
                    if t < 4:
                        pltpu.make_async_copy(source(t, 0), target(t, r), recv_sem.at[t, r]).wait()
                    else:
                        @pl.when(r != me)
                        def _():
                            pltpu.make_async_copy(source(t, 0), target(t, r), recv_sem.at[t, r]).wait()
                return 0
            lax.fori_loop(0, N_CP, one, 0)

        arrive((1, 2, 4))
        lse = jnp.concatenate([s_buf[i, 0:1, :] for i in range(N_CP)], axis=1)

        def value_step(i, _):
            b = block_at(i)
            us = pl.ds(b * UB, UB)
            arrive_pair(0, b)
            k = k_buf[us].reshape(UB * rows, SPAN)
            st = lax.dot_general(k, q_buf[...].reshape(seq, SPAN), NT, preferred_element_type=F32)
            p = jnp.exp2(st * (scale * LOG2E) - lse)
            prob[pl.ds(pl.multiple_of(b * UB * rows, UB * rows), UB * rows), :] = p
            dv = jnp.dot(p.astype(BF16), g_buf[...].reshape(seq, SPAN), preferred_element_type=F32)
            done[0, us] = dv.astype(BF16).reshape(UB, rows, SPAN)
            give(0, 2 * b)
            give(0, 2 * b + 1)
            return 0

        lax.fori_loop(0, N_CP // UB, value_step, 0)
        dq_acc[...] = jnp.zeros_like(dq_acc)


    def key_step(i):
        b = block_at(i)
        us = pl.ds(b * UB, UB)
        arrive_pair(3, b)
        k = k_buf[us].reshape(UB * rows, SPAN)
        v = v_buf[us].reshape(UB * rows, SPAN)
        delta = jnp.concatenate([s_buf[i, 1:2, :] for i in range(N_CP)], axis=1)
        p = prob[pl.ds(pl.multiple_of(b * UB * rows, UB * rows), UB * rows), :]
        dp = lax.dot_general(v, g_buf[...].reshape(seq, SPAN), NT, preferred_element_type=F32)
        ds = (p * (dp - delta)).astype(BF16)
        dk = jnp.dot(ds, q_buf[...].reshape(seq, SPAN), preferred_element_type=F32)
        done[1, us] = (dk * scale).astype(BF16).reshape(UB, rows, SPAN)
        dq_acc[...] += lax.dot_general(ds, k, TN, preferred_element_type=F32)
        give(1, 2 * b)
        give(1, 2 * b + 1)

    def key_or_pass(i, _):
        @pl.when(active)
        def _():
            key_step(i)

        pass_on(i, 0)
        return 0

    lax.fori_loop(0, N_Z, key_or_pass, 0)

    @pl.when(active)
    def _():
        done[2] = (dq_acc[...] * scale).astype(BF16).reshape(N_CP, rows, SPAN)

        def query_give(i, _):
            b = block_at(i)
            give(2, 2 * b)
            give(2, 2 * b + 1)
            return 0

        lax.fori_loop(0, N_Z, query_give, 0)

    outs = (dv_out, dk_out, dq_out)

    def collect_all(t):
        def collect(h, _):
            @pl.when(h != mine)
            def _():
                pltpu.make_async_copy(done.at[t, 0], back.at[t, :, cols_of(h)], ret_recv.at[t, h]).wait()
            return 0

        lax.fori_loop(0, HEADS, collect, 0)
        pltpu.make_async_copy(back.at[t], outs[t].at[0], out_sem.at[t]).start()

    lax.fori_loop(N_Z, HEADS, pass_on, 0)
    pltpu.make_async_copy(back.at[0], outs[0].at[0], out_sem.at[0]).start()
    dv_buf[my_rows, :] = back[0, :, pl.ds(pl.multiple_of(y0 * half_w, half_w), half_w)]
    for j in range(1, 4):
        feature_copy(j).wait()

    def values_from(i, _):
        from_y, at = lax.rem(y + 1 + i // half_h, 4), lax.rem(i, half_h)
        rs = pl.ds(pl.multiple_of(from_y * SPAN, SPAN), SPAN)
        pltpu.make_async_copy(
            back.at[0, :, cols_of(at)], dv_buf.at[rs, cols_of(at)], y_rsem.at[from_y, at]).wait()
        return 0

    lax.fori_loop(0, 3 * half_h, values_from, 0)

    def part_of(which, j):
        at = pl.multiple_of((lax.rem(j, 2) * 2 + which) * blk, blk)
        return jnp.dot(ft_buf[j // 2, pl.ds(at, blk), :], dv_buf[...], preferred_element_type=F32)

    def half_copy(j):
        return pltpu.make_async_remote_copy(
            src_ref=half_send.at[j], dst_ref=half_recv.at[j], send_sem=d_ssem.at[j],
            recv_sem=d_rsem.at[j], device_id={"core": 1 - core}, device_id_type=MESH)

    rows_x = blk // 2

    def x_copy(c, j):
        rs = pl.ds(c * rows_x, rows_x)
        return pltpu.make_async_remote_copy(
            src_ref=x_send.at[j, rs], dst_ref=x_recv.at[x, rs], send_sem=x_ssem.at[c, j],
            recv_sem=x_rsem.at[c, x], device_id=row_id(j), device_id_type=MESH)


    def to_other(o, _):
        j = lax.rem(x + 1 + o, 4)
        half_send[j] = part_of(1 - core, j).astype(BF16)
        half_copy(j).start()
        return 0

    def to_owner(o, _):
        j = lax.rem(x + 1 + o, 4)
        part[...] = part_of(core, j)
        half_copy(j).wait_recv()
        both = (part[...] + half_recv[j].astype(F32)).astype(BF16)

        @pl.when(j == x)
        def _():
            x_recv[x] = both

        @pl.when(j != x)
        def _():
            x_send[j] = both
            x_copy(0, j).start()
        return 0

    lax.fori_loop(0, 4, to_other, 0)
    lax.fori_loop(0, 4, to_owner, 0)
    for o in range(1, 4):
        x_copy(1, lax.rem(x + o, 4)).start()

    def z_copy(c, zz):
        return pltpu.make_async_remote_copy(
            src_ref=z_send.at[c, zz], dst_ref=z_recv.at[c, z], send_sem=z_ssem.at[c, zz],
            recv_sem=z_rsem.at[c, z], device_id=owner_id(zz), device_id_type=MESH)

    def is_here(zz):
        return jnp.logical_and(stays, zz == z)

    gap = jnp.zeros((rows_x, SPAN - col), BF16)
    for c in range(2):
        for o in range(1, 4):
            s = lax.rem(x + o, 4)
            rs = pl.ds(c * rows_x, rows_x)
            pltpu.make_async_copy(x_send.at[s, rs], x_recv.at[s, rs], x_rsem.at[c, s]).wait()
        both = x_recv[0, c * rows_x : (c + 1) * rows_x].astype(F32)
        for s in range(1, 4):
            both += x_recv[s, c * rows_x : (c + 1) * rows_x].astype(F32)
        for zz in range(N_Z):
            piece = both[:, zz * col : (zz + 1) * col].astype(BF16)
            z_send[c, zz] = jnp.concatenate([piece, gap], axis=1)

        def z_start(i, _):
            zz = lax.rem(z + far_first(i), N_Z)

            @pl.when(jnp.logical_not(is_here(zz)))
            def _():
                z_copy(c, zz).start()

            @pl.when(is_here(zz))
            def _():
                z_recv[c, zz] = z_send[c, zz]
            return 0

        lax.fori_loop(0, N_Z, z_start, 0)
    collect_all(1)
    collect_all(2)
    total[...] = jnp.zeros_like(total)
    for c in range(2):
        def z_take(i, _):
            zz = lax.rem(z + far_first(i), N_Z)

            @pl.when(jnp.logical_not(is_here(zz)))
            def _():
                pltpu.make_async_copy(
                    z_send.at[c, zz], z_recv.at[c, zz], z_rsem.at[c, zz]).wait()

            total[c * rows_x : (c + 1) * rows_x] += z_recv[c, zz][:, :col].astype(F32)
            return 0

        lax.fori_loop(0, N_Z, z_take, 0)
    last = pltpu.make_async_copy(total, dw_out, out_sem.at[3])
    last.start()

    def sent(head, _):
        @pl.when(head != mine)
        def _():
            for t in range(5):
                pltpu.make_async_copy(source(t, head), target(t, me), send_sem.at[t, head]).wait()
        return 0

    lax.fori_loop(0, HEADS, sent, 0)

    @pl.when(active)
    def _():
        def gave(j, _):
            peer = lax.rem(me + j, N_CP)
            for t in range(3):
                pltpu.make_async_copy(
                    done.at[t, peer], back.at[t, :, cols_of(mine)], ret_send.at[t, peer]).wait()
            return 0

        lax.fori_loop(1, N_CP, gave, 0)

    def passed(h, _):
        for o in range(2):
            to, copy = value_copy(h, o)

            @pl.when(to != y)
            def _():
                copy.wait_send()
        return 0

    lax.fori_loop(0, HEADS, passed, 0)

    def x_sent(j, _):
        half_copy(j).wait_send()

        @pl.when(j != x)
        def _():
            for c in range(2):
                x_copy(c, j).wait_send()
        return 0

    lax.fori_loop(0, 4, x_sent, 0)

    def z_sent(zz, _):
        @pl.when(jnp.logical_not(is_here(zz)))
        def _():
            for c in range(2):
                z_copy(c, zz).wait_send()
        return 0

    lax.fori_loop(0, N_Z, z_sent, 0)
    for t in range(3):
        pltpu.make_async_copy(back.at[t], outs[t].at[0], out_sem.at[t]).wait()
    last.wait()


def on_device(features, query_rows, key_rows, value_rows, attn_output, grad_output, log_sums):
    _, rows, width = query_rows.shape
    feat = features.shape[2]
    seq = N_CP * rows
    blk, half_w = feat // 16, width // 2
    any_spec = pl.BlockSpec(memory_space=pl.ANY)
    block = pltpu.VMEM((N_CP, rows, SPAN), BF16)
    out = jax.ShapeDtypeStruct(query_rows.shape, BF16)
    dma = pltpu.SemaphoreType.DMA
    return pl.pallas_call(
        functools.partial(step_kernel, scale=SPAN**-0.5, rows=rows),
        out_shape=(out, out, out, jax.ShapeDtypeStruct((blk, half_w // N_Z), F32)),
        in_specs=[any_spec] * 7,
        out_specs=(any_spec,) * 4,
        scratch_shapes=[
            block, block, block, block,
            pltpu.VMEM((N_CP, 8, rows), F32),
            pltpu.VMEM((seq, seq), F32),
            pltpu.VMEM((seq, SPAN), F32),
            pltpu.VMEM((3, N_CP, rows, SPAN), BF16),
            pltpu.VMEM((3, rows, width), BF16),
            pltpu.VMEM((rows, width), BF16),
            pltpu.VMEM((rows, width), BF16),
            pltpu.VMEM((HEADS, 1, rows), F32),
            pltpu.VMEM((HEADS, 8, rows), F32),
            pltpu.VMEM((rows, feat), BF16),
            pltpu.VMEM((2, 2, feat // 4, rows), BF16),
            pltpu.VMEM((2, feat // 4, 4 * rows), BF16),
            pltpu.VMEM((4 * rows, half_w), BF16),
            pltpu.VMEM((4, blk, half_w), BF16),
            pltpu.VMEM((4, blk, half_w), BF16),
            pltpu.VMEM((blk, half_w), F32),
            pltpu.VMEM((4, blk, half_w), BF16),
            pltpu.VMEM((4, blk, half_w), BF16),
            pltpu.VMEM((2, N_Z, blk // 2, SPAN), BF16),
            pltpu.VMEM((2, N_Z, blk // 2, SPAN), BF16),
            pltpu.VMEM((blk, half_w // N_Z), F32),
            dma((4,)),
            dma((5, HEADS)), dma((5, N_CP)), dma((3, N_CP)), dma((3, HEADS)), dma((4,)),
            dma((4,)), dma((4,)), dma((HEADS, 2)), dma((4, HEADS // 2)), dma((4,)), dma((4,)),
            dma((2, 4)), dma((2, 4)), dma((2, N_Z)), dma((2, N_Z)),
        ],
        compiler_params=pltpu.CompilerParams(
            collective_id=0, has_side_effects=True, vmem_limit_bytes=60 * 2**20),
        name="step",
    )(features, query_rows, key_rows, value_rows, attn_output, grad_output,
      jnp.transpose(log_sums, (2, 0, 1)))


def solution(mesh):
    finer = Mesh(mesh.devices.reshape(2, 4, 2, 2, 8), AXES)
    rows = P(FSDP, CP, None)
    return jax.shard_map(
        on_device, mesh=finer, in_specs=(rows,) * 7,
        out_specs=(rows, rows, rows, P(FSDP, CP)), check_vma=False,
    )
```

time: 109 us -> 99.9 us (0.917)
  the two profiles are of different devices: /device:TPU:4 before, /device:TPU:19 now
where the time goes in v3:
time: 99.9 us; the launch traced here: 98 us
  Pallas kernels  93 us (93%)
  local copies, waits for them, and re-layouts  4.43 us (4%)
    pallas_call x1, Pallas kernels, on_device(): pl.pallas_call(functools.partial(step_kernel, scale=SPAN ** (-0.5), rows=...  93 us
    unnamed x10, local copies, waits for them, and re-layouts  4.43 us

profile of v3, /device:TPU:19, one launch (start us, length us, event | category | flops | bytes accessed | tf_op | source)
XLA Modules:
  0.0 98.0 jit_solution(17290704007020930507)
XLA Ops:
  0.6 93.0 %step.1 = (bf16[1,128,1280]{2,1,0:T(8,128)(2,1)}, bf16[1,128,1280]{2,1,0:T(8,128)(2,1)}, bf16[1,128,1280]{2,1,0:T(8,128)(2,1)}, f32[160,80]{1,0:T(8,128)}) custom-call(bf16[1,128,2560]{2,1,0:T(8,128)(2,1)} %f_in.1, bf16[1,128,1280]{2,1,0:T(8,128)(2,1)} %q_in.1, bf16[1,128,1280]{2,1,0:T(8,128)(2,1)} %k_in.1, bf16[1,128,1280]{2,1,0:T(8,128)(2,1)} %v_in.1, ...), custom_call_target="tpu_custom_call" | custom-call | tf_op jit(solution)/shard_map/step/pallas_call | solution.py:499
  93.6 0.0 copy-start.1
  93.6 1.8 %copy.15 = bf16[1,128,1280]{2,1,0:T(8,128)(2,1)} copy(bf16[1,128,1280]{2,1,0:T(8,128)(2,1)} %get-tuple-element.8) | data formatting | bytes 655360
  95.4 0.0 copy-done.1
  95.4 0.0 copy-start
  95.4 0.7 copy.16
  96.1 0.4 copy-done
  96.5 0.0 copy-start.2
  96.5 0.7 copy.17
  97.2 0.2 copy-done.2
  97.4 0.6 copy.18
Async XLA Ops:
  93.6 1.8 %copy-start.1 = (bf16[1,128,1280]{2,1,0:T(8,128)(2,1)S(1)}, bf16[1,128,1280]{2,1,0:T(8,128)(2,1)}, u32[]{:S(2)}) copy-start(bf16[1,128,1280]{2,1,0:T(8,128)(2,1)} %get-tuple-element.9) | copy-start | bytes 983044
  95.4 1.1 %copy-start = (bf16[1,128,1280]{2,1,0:T(8,128)(2,1)S(1)}, bf16[1,128,1280]{2,1,0:T(8,128)(2,1)}, u32[]{:S(2)}) copy-start(bf16[1,128,1280]{2,1,0:T(8,128)(2,1)} %get-tuple-element.10) | copy-start | bytes 983044
  96.5 0.9 copy-start.2

commit v4 on v3

--- a/solution.py
+++ b/solution.py
@@ -13,6 +13,7 @@
 CP = ("x_lo", "z")
 LOG2E = 1.4426950408889634
 HEADS = 10
+HALF = HEADS // 2
 SPAN = 128
 N_CP = 16
 N_Z = 8
@@ -39,7 +40,7 @@
 def step_kernel(
     f_in, q_in, k_in, v_in, o_in, g_in, l_in, dq_out, dk_out, dv_out, dw_out,
     q_buf, k_buf, v_buf, g_buf, s_buf, prob, dq_acc, done, back,
-    g_own, o_own, l_own, s_own, f_own, ft_own, ft_buf, dv_buf,
+    g_own, o_own, l_own, s_own, f_own, ft_own, ft_out, ft_buf, dv_buf,
     half_send, half_recv, part, x_send, x_recv, z_send, z_recv, total,
     in_sem, send_sem, recv_sem, ret_send, ret_recv, out_sem,
     f_ssem, f_rsem, y_ssem, y_rsem, d_ssem, d_rsem, x_ssem, x_rsem, z_ssem, z_rsem,
@@ -54,20 +55,20 @@
     feat = f_in.shape[2]
     half_w = q_in.shape[2] // 2
     blk = feat // 16
-    per = feat // 4 // SPAN
+    piece = blk // 2
     col = half_w // N_Z
 
     def cp_id(peer):
         return {"x_lo": lax.rem(peer, 2), "z": peer // 2}
 
-    y1, y0 = y // 2, lax.rem(y, 2)
-    stays = y0 == xl
-
     def row_id(p):
         return {"x_hi": p // 2, "x_lo": lax.rem(p, 2)}
 
-    def owner_id(zz):
-        return {"x_lo": y0, "y": 2 * y1 + xl, "z": zz}
+    def y_id(p):
+        return {"y": p}
+
+    near, near_id = (y, x), (y_id, row_id)
+    across, across_id = (x, y), (row_id, y_id)
 
     loads = [
         pltpu.make_async_copy(g_in.at[0], g_own, in_sem.at[0]),
@@ -92,18 +93,10 @@
         signal(row_id(lax.rem(x + j, 4)))
         return 0
 
-    def greet_owner(zz, _):
-        signal(owner_id(zz))
-        return 0
-
-    @pl.when(jnp.logical_not(stays))
-    def _():
-        lax.fori_loop(0, N_Z, greet_owner, 0)
-
     lax.fori_loop(1, N_CP, greet_cp, 0)
     lax.fori_loop(1, 4, greet_quad, 0)
     signal({"core": 1 - core})
-    pl.semaphore_wait(barrier, jnp.where(stays, 22, 30))
+    pl.semaphore_wait(barrier, N_CP + 6)
 
     def far_first(i):
         return jnp.where(lax.rem(i, 2) == 0, 4 + i // 2, 3 - i // 2) % N_Z
@@ -161,40 +154,61 @@
         s_own[h, 1:2, :] = jnp.sum(product.T, axis=0, keepdims=True)
     send_all((4,))
     send_all((0,))
-    send_all((3,))
 
     loads[3].wait()
 
     def turn(i, _):
         at = pl.multiple_of(i * SPAN, SPAN)
-        group = i // per
-        rs = pl.ds(pl.multiple_of(lax.rem(i, per) * SPAN, SPAN), SPAN)
-        ft_own[group // 2, lax.rem(group, 2), rs, :] = f_own[:, pl.ds(at, SPAN)].T
+        ft_own[pl.ds(at, SPAN), :] = f_own[:, pl.ds(at, SPAN)].T
         return 0
 
     lax.fori_loop(0, feat // SPAN, turn, 0)
-    my_rows = pl.ds(pl.multiple_of(y * SPAN, SPAN), SPAN)
-
-    def feature_copy(j):
-        to = lax.rem(y + j, 4)
+
+    def sort(i, _):
+        f, part_s = i // 2, lax.rem(i, 2)
+        of_y, of_x, of_core = lax.rem(f // 2, 4), 2 * (f // 8) + part_s, lax.rem(f, 2)
+        value = ft_own[pl.ds(pl.multiple_of(i * piece, piece), piece), :]
+        ft_out[0, of_y, pl.ds(pl.multiple_of((of_core * 4 + of_x) * piece, piece), piece), :] = value
+        ft_out[1, of_x, pl.ds(pl.multiple_of((of_core * 4 + of_y) * piece, piece), piece), :] = value
+        return 0
+
+    lax.fori_loop(0, feat // piece, sort, 0)
+
+    def my_span(w):
+        return pl.ds(pl.multiple_of(near[w] * SPAN, SPAN), SPAN)
+
+    def feature_copy(w, j):
+        to = lax.rem(near[w] + j, 4)
         return pltpu.make_async_remote_copy(
-            src_ref=ft_own.at[:, to // 2], dst_ref=ft_buf.at[:, :, my_rows],
-            send_sem=f_ssem.at[j], recv_sem=f_rsem.at[j], device_id={"y": to},
+            src_ref=ft_out.at[w, to], dst_ref=ft_buf.at[w, :, my_span(w)],
+            send_sem=f_ssem.at[w, j], recv_sem=f_rsem.at[w, j], device_id=near_id[w](to),
             device_id_type=MESH)
 
-    for j in range(1, 4):
-        feature_copy(j).start()
-    ft_buf[:, :, my_rows] = ft_own[:, y1]
-
-    half_h = HEADS // 2
-
-    def value_copy(h, o):
-        to = h // half_h + 2 * o
-        at = lax.rem(h, half_h)
-        return to, pltpu.make_async_remote_copy(
-            src_ref=back.at[0, :, cols_of(h)], dst_ref=dv_buf.at[my_rows, cols_of(at)],
-            send_sem=y_ssem.at[h, o], recv_sem=y_rsem.at[y, at], device_id={"y": to},
-            device_id_type=MESH)
+    for w in range(2):
+        for j in range(1, 4):
+            feature_copy(w, j).start()
+        ft_buf[w, :, my_span(w)] = ft_out[w, near[w]]
+
+    def left(kinds):
+        def one(head, _):
+            @pl.when(head != mine)
+            def _():
+                for t in kinds:
+                    pltpu.make_async_copy(source(t, head), target(t, me), send_sem.at[t, head]).wait()
+            return 0
+
+        lax.fori_loop(0, HEADS, one, 0)
+
+    left((1, 2))
+    left((0,))
+    send_all((3,))
+
+    def value_copy(w, h, o):
+        return pltpu.make_async_remote_copy(
+            src_ref=back.at[0, :, cols_of(h)],
+            dst_ref=dv_buf.at[w, my_span(w), cols_of(h - HALF * w)],
+            send_sem=y_ssem.at[h, o], recv_sem=y_rsem.at[near[w], h],
+            device_id=near_id[w](lax.rem(near[w] + o, 4)), device_id_type=MESH)
 
     def pass_on(i, _):
         h = jnp.where(i < N_Z, lax.rem(z + far_first(i), N_Z), i)
@@ -203,12 +217,11 @@
         def _():
             pltpu.make_async_copy(done.at[0, 0], back.at[0, :, cols_of(h)], ret_recv.at[0, h]).wait()
 
-        for o in range(2):
-            to, copy = value_copy(h, o)
-
-            @pl.when(to != y)
-            def _():
-                copy.start()
+        for w in range(2):
+            @pl.when(h // HALF == w)
+            def _():
+                for o in range(1, 4):
+                    value_copy(w, h, o).start()
         return 0
 
     UB = 2
@@ -285,18 +298,16 @@
         give(1, 2 * b)
         give(1, 2 * b + 1)
 
-    def key_or_pass(i, _):
-        @pl.when(active)
-        def _():
-            key_step(i)
-
-        pass_on(i, 0)
-        return 0
-
-    lax.fori_loop(0, N_Z, key_or_pass, 0)
-
-    @pl.when(active)
-    def _():
+    def key_steps(lo, hi):
+        def one(i, _):
+            @pl.when(active)
+            def _():
+                key_step(i)
+            return 0
+
+        lax.fori_loop(lo, hi, one, 0)
+
+    def finish_queries():
         done[2] = (dq_acc[...] * scale).astype(BF16).reshape(N_CP, rows, SPAN)
 
         def query_give(i, _):
@@ -307,6 +318,13 @@
 
         lax.fori_loop(0, N_Z, query_give, 0)
 
+    def passes(lo, hi):
+        lax.fori_loop(lo, hi, pass_on, 0)
+
+    passes(0, HEADS)
+    key_steps(0, N_Z)
+    pl.when(active)(finish_queries)
+
     outs = (dv_out, dk_out, dq_out)
 
     def collect_all(t):
@@ -319,128 +337,89 @@
         lax.fori_loop(0, HEADS, collect, 0)
         pltpu.make_async_copy(back.at[t], outs[t].at[0], out_sem.at[t]).start()
 
-    lax.fori_loop(N_Z, HEADS, pass_on, 0)
     pltpu.make_async_copy(back.at[0], outs[0].at[0], out_sem.at[0]).start()
-    dv_buf[my_rows, :] = back[0, :, pl.ds(pl.multiple_of(y0 * half_w, half_w), half_w)]
-    for j in range(1, 4):
-        feature_copy(j).wait()
-
-    def values_from(i, _):
-        from_y, at = lax.rem(y + 1 + i // half_h, 4), lax.rem(i, half_h)
-        rs = pl.ds(pl.multiple_of(from_y * SPAN, SPAN), SPAN)
-        pltpu.make_async_copy(
-            back.at[0, :, cols_of(at)], dv_buf.at[rs, cols_of(at)], y_rsem.at[from_y, at]).wait()
-        return 0
-
-    lax.fori_loop(0, 3 * half_h, values_from, 0)
-
-    def part_of(which, j):
-        at = pl.multiple_of((lax.rem(j, 2) * 2 + which) * blk, blk)
-        return jnp.dot(ft_buf[j // 2, pl.ds(at, blk), :], dv_buf[...], preferred_element_type=F32)
-
-    def half_copy(j):
+
+    for w in range(2):
+        dv_buf[w, my_span(w), :] = back[0, :, w * half_w : (w + 1) * half_w]
+    for w in range(2):
+        for j in range(1, 4):
+            feature_copy(w, j).wait()
+
+    def values_from(w):
+        def one(i, _):
+            source_at, at = lax.rem(near[w] + 1 + i // HALF, 4), lax.rem(i, HALF)
+            rs = pl.ds(pl.multiple_of(source_at * SPAN, SPAN), SPAN)
+            pltpu.make_async_copy(
+                back.at[0, :, cols_of(at)], dv_buf.at[w, rs, cols_of(at)],
+                y_rsem.at[source_at, HALF * w + at]).wait()
+            return 0
+
+        lax.fori_loop(0, 3 * HALF, one, 0)
+
+    def part_of(w, which):
+        rs = pl.ds(pl.multiple_of(which * 2 * blk, 2 * blk), 2 * blk)
+        return jnp.dot(ft_buf[w, rs, :], dv_buf[w], preferred_element_type=F32)
+
+    def half_copy(w):
         return pltpu.make_async_remote_copy(
-            src_ref=half_send.at[j], dst_ref=half_recv.at[j], send_sem=d_ssem.at[j],
-            recv_sem=d_rsem.at[j], device_id={"core": 1 - core}, device_id_type=MESH)
-
-    rows_x = blk // 2
-
-    def x_copy(c, j):
-        rs = pl.ds(c * rows_x, rows_x)
+            src_ref=half_send.at[w], dst_ref=half_recv.at[w], send_sem=d_ssem.at[w],
+            recv_sem=d_rsem.at[w], device_id={"core": 1 - core}, device_id_type=MESH)
+
+    def across_copy(w, j):
         return pltpu.make_async_remote_copy(
-            src_ref=x_send.at[j, rs], dst_ref=x_recv.at[x, rs], send_sem=x_ssem.at[c, j],
-            recv_sem=x_rsem.at[c, x], device_id=row_id(j), device_id_type=MESH)
-
-
-    def to_other(o, _):
-        j = lax.rem(x + 1 + o, 4)
-        half_send[j] = part_of(1 - core, j).astype(BF16)
-        half_copy(j).start()
-        return 0
-
-    def to_owner(o, _):
-        j = lax.rem(x + 1 + o, 4)
-        part[...] = part_of(core, j)
-        half_copy(j).wait_recv()
-        both = (part[...] + half_recv[j].astype(F32)).astype(BF16)
-
-        @pl.when(j == x)
-        def _():
-            x_recv[x] = both
-
-        @pl.when(j != x)
-        def _():
-            x_send[j] = both
-            x_copy(0, j).start()
-        return 0
-
-    lax.fori_loop(0, 4, to_other, 0)
-    lax.fori_loop(0, 4, to_owner, 0)
-    for o in range(1, 4):
-        x_copy(1, lax.rem(x + o, 4)).start()
-
-    def z_copy(c, zz):
+            src_ref=x_send.at[w, j], dst_ref=x_recv.at[w, across[w]], send_sem=x_ssem.at[w, j],
+            recv_sem=x_rsem.at[w, across[w]], device_id=across_id[w](j), device_id_type=MESH)
+
+    for w in range(2):
+        values_from(w)
+        half_send[w] = part_of(w, 1 - core).astype(BF16)
+        half_copy(w).start()
+    for w in range(2):
+        part[...] = part_of(w, core)
+        half_copy(w).wait_recv()
+        both = (part[...] + half_recv[w].astype(F32)).astype(BF16)
+        x_send[w] = both.reshape(4, piece, half_w)
+        for o in range(1, 4):
+            across_copy(w, lax.rem(across[w] + o, 4)).start()
+        x_recv[w, across[w]] = x_send[w, across[w]]
+
+    def z_copy(w, zz):
         return pltpu.make_async_remote_copy(
-            src_ref=z_send.at[c, zz], dst_ref=z_recv.at[c, z], send_sem=z_ssem.at[c, zz],
-            recv_sem=z_rsem.at[c, z], device_id=owner_id(zz), device_id_type=MESH)
-
-    def is_here(zz):
-        return jnp.logical_and(stays, zz == z)
-
-    gap = jnp.zeros((rows_x, SPAN - col), BF16)
-    for c in range(2):
+            src_ref=z_send.at[w, zz], dst_ref=z_recv.at[xl, z], send_sem=z_ssem.at[w, zz],
+            recv_sem=z_rsem.at[xl, z], device_id={"x_lo": w, "z": zz}, device_id_type=MESH)
+
+    def is_here(w, zz):
+        return jnp.logical_and(xl == w, zz == z)
+
+    gap = jnp.zeros((piece, SPAN - col), BF16)
+    for w in range(2):
         for o in range(1, 4):
-            s = lax.rem(x + o, 4)
-            rs = pl.ds(c * rows_x, rows_x)
-            pltpu.make_async_copy(x_send.at[s, rs], x_recv.at[s, rs], x_rsem.at[c, s]).wait()
-        both = x_recv[0, c * rows_x : (c + 1) * rows_x].astype(F32)
+            s = lax.rem(across[w] + o, 4)
+            pltpu.make_async_copy(x_send.at[w, s], x_recv.at[w, s], x_rsem.at[w, s]).wait()
+        both = x_recv[w, 0].astype(F32)
         for s in range(1, 4):
-            both += x_recv[s, c * rows_x : (c + 1) * rows_x].astype(F32)
+            both += x_recv[w, s].astype(F32)
         for zz in range(N_Z):
-            piece = both[:, zz * col : (zz + 1) * col].astype(BF16)
-            z_send[c, zz] = jnp.concatenate([piece, gap], axis=1)
+            block16 = both[:, zz * col : (zz + 1) * col].astype(BF16)
+            z_send[w, zz] = jnp.concatenate([block16, gap], axis=1)
 
         def z_start(i, _):
             zz = lax.rem(z + far_first(i), N_Z)
 
-            @pl.when(jnp.logical_not(is_here(zz)))
-            def _():
-                z_copy(c, zz).start()
-
-            @pl.when(is_here(zz))
-            def _():
-                z_recv[c, zz] = z_send[c, zz]
+            @pl.when(jnp.logical_not(is_here(w, zz)))
+            def _():
+                z_copy(w, zz).start()
+
+            @pl.when(is_here(w, zz))
+            def _():
+                z_recv[xl, zz] = z_send[w, zz]
             return 0
 
         lax.fori_loop(0, N_Z, z_start, 0)
+
     collect_all(1)
     collect_all(2)
-    total[...] = jnp.zeros_like(total)
-    for c in range(2):
-        def z_take(i, _):
-            zz = lax.rem(z + far_first(i), N_Z)
-
-            @pl.when(jnp.logical_not(is_here(zz)))
-            def _():
-                pltpu.make_async_copy(
-                    z_send.at[c, zz], z_recv.at[c, zz], z_rsem.at[c, zz]).wait()
-
-            total[c * rows_x : (c + 1) * rows_x] += z_recv[c, zz][:, :col].astype(F32)
-            return 0
-
-        lax.fori_loop(0, N_Z, z_take, 0)
-    last = pltpu.make_async_copy(total, dw_out, out_sem.at[3])
-    last.start()
-
-    def sent(head, _):
-        @pl.when(head != mine)
-        def _():
-            for t in range(5):
-                pltpu.make_async_copy(source(t, head), target(t, me), send_sem.at[t, head]).wait()
-        return 0
-
-    lax.fori_loop(0, HEADS, sent, 0)
-
+    left((4, 3))
     @pl.when(active)
     def _():
         def gave(j, _):
@@ -453,32 +432,40 @@
         lax.fori_loop(1, N_CP, gave, 0)
 
     def passed(h, _):
-        for o in range(2):
-            to, copy = value_copy(h, o)
-
-            @pl.when(to != y)
-            def _():
-                copy.wait_send()
+        for w in range(2):
+            @pl.when(h // HALF == w)
+            def _():
+                for o in range(1, 4):
+                    value_copy(w, h, o).wait_send()
         return 0
 
     lax.fori_loop(0, HEADS, passed, 0)
-
-    def x_sent(j, _):
-        half_copy(j).wait_send()
-
-        @pl.when(j != x)
-        def _():
-            for c in range(2):
-                x_copy(c, j).wait_send()
-        return 0
-
-    lax.fori_loop(0, 4, x_sent, 0)
+    for w in range(2):
+        half_copy(w).wait_send()
+        for o in range(1, 4):
+            across_copy(w, lax.rem(across[w] + o, 4)).wait_send()
+
+    total[...] = jnp.zeros_like(total)
+    for xs in range(2):
+        def take(i, _):
+            zz = lax.rem(z + far_first(i), N_Z)
+
+            @pl.when(jnp.logical_not(jnp.logical_and(xl == xs, zz == z)))
+            def _():
+                pltpu.make_async_copy(z_send.at[0, zz], z_recv.at[xs, zz], z_rsem.at[xs, zz]).wait()
+
+            total[xs * piece : (xs + 1) * piece] += z_recv[xs, zz][:, :col].astype(F32)
+            return 0
+
+        lax.fori_loop(0, N_Z, take, 0)
+    last = pltpu.make_async_copy(total, dw_out, out_sem.at[3])
+    last.start()
 
     def z_sent(zz, _):
-        @pl.when(jnp.logical_not(is_here(zz)))
-        def _():
-            for c in range(2):
-                z_copy(c, zz).wait_send()
+        for w in range(2):
+            @pl.when(jnp.logical_not(is_here(w, zz)))
+            def _():
+                z_copy(w, zz).wait_send()
         return 0
 
     lax.fori_loop(0, N_Z, z_sent, 0)
@@ -513,20 +500,21 @@
             pltpu.VMEM((HEADS, 1, rows), F32),
             pltpu.VMEM((HEADS, 8, rows), F32),
             pltpu.VMEM((rows, feat), BF16),
-            pltpu.VMEM((2, 2, feat // 4, rows), BF16),
+            pltpu.VMEM((feat, rows), BF16),
+            pltpu.VMEM((2, 4, feat // 4, rows), BF16),
             pltpu.VMEM((2, feat // 4, 4 * rows), BF16),
-            pltpu.VMEM((4 * rows, half_w), BF16),
-            pltpu.VMEM((4, blk, half_w), BF16),
-            pltpu.VMEM((4, blk, half_w), BF16),
-            pltpu.VMEM((blk, half_w), F32),
-            pltpu.VMEM((4, blk, half_w), BF16),
-            pltpu.VMEM((4, blk, half_w), BF16),
+            pltpu.VMEM((2, 4 * rows, half_w), BF16),
+            pltpu.VMEM((2, 2 * blk, half_w), BF16),
+            pltpu.VMEM((2, 2 * blk, half_w), BF16),
+            pltpu.VMEM((2 * blk, half_w), F32),
+            pltpu.VMEM((2, 4, blk // 2, half_w), BF16),
+            pltpu.VMEM((2, 4, blk // 2, half_w), BF16),
             pltpu.VMEM((2, N_Z, blk // 2, SPAN), BF16),
             pltpu.VMEM((2, N_Z, blk // 2, SPAN), BF16),
             pltpu.VMEM((blk, half_w // N_Z), F32),
             dma((4,)),
             dma((5, HEADS)), dma((5, N_CP)), dma((3, N_CP)), dma((3, HEADS)), dma((4,)),
-            dma((4,)), dma((4,)), dma((HEADS, 2)), dma((4, HEADS // 2)), dma((4,)), dma((4,)),
+            dma((2, 4)), dma((2, 4)), dma((HEADS, 4)), dma((4, HEADS)), dma((2,)), dma((2,)),
             dma((2, 4)), dma((2, 4)), dma((2, N_Z)), dma((2, N_Z)),
         ],
         compiler_params=pltpu.CompilerParams(

time: 99.9 us -> 94.3 us (0.944); the launches traced: 98 us -> 94.2 us
  Pallas kernels: 93 us -> 89.1 us
    pallas_call x1, Pallas kernels: 93 us -> 89.1 us  [on_device(): pl.pallas_call(functools.partial(step_kernel, scale=SPAN ** (-0.5), rows=...]
where the time goes in v4:
time: 94.3 us; the launch traced here: 94.2 us
  Pallas kernels  89.1 us (94%)
  local copies, waits for them, and re-layouts  4.43 us (5%)
    pallas_call x1, Pallas kernels, on_device(): pl.pallas_call(functools.partial(step_kernel, scale=SPAN ** (-0.5), rows=...  89.1 us
    unnamed x10, local copies, waits for them, and re-layouts  4.43 us

profile of v4, /device:TPU:19, one launch (start us, length us, event | category | flops | bytes accessed | tf_op | source)
XLA Modules:
  0.0 94.2 jit_solution(3626635112409653331)
XLA Ops:
  0.6 89.1 %step.1 = (bf16[1,128,1280]{2,1,0:T(8,128)(2,1)}, bf16[1,128,1280]{2,1,0:T(8,128)(2,1)}, bf16[1,128,1280]{2,1,0:T(8,128)(2,1)}, f32[160,80]{1,0:T(8,128)}) custom-call(bf16[1,128,2560]{2,1,0:T(8,128)(2,1)} %f_in.1, bf16[1,128,1280]{2,1,0:T(8,128)(2,1)} %q_in.1, bf16[1,128,1280]{2,1,0:T(8,128)(2,1)} %k_in.1, bf16[1,128,1280]{2,1,0:T(8,128)(2,1)} %v_in.1, ...), custom_call_target="tpu_custom_call" | custom-call | tf_op jit(solution)/shard_map/step/pallas_call | solution.py:486
  89.7 0.0 copy-start.1
  89.7 1.8 %copy.15 = bf16[1,128,1280]{2,1,0:T(8,128)(2,1)} copy(bf16[1,128,1280]{2,1,0:T(8,128)(2,1)} %get-tuple-element.8) | data formatting | bytes 655360
  91.5 0.0 copy-done.1
  91.5 0.0 copy-start
  91.5 0.7 copy.16
  92.2 0.4 copy-done
  92.6 0.0 copy-start.2
  92.6 0.7 copy.17
  93.3 0.2 copy-done.2
  93.5 0.6 copy.18
Async XLA Ops:
  89.7 1.8 %copy-start.1 = (bf16[1,128,1280]{2,1,0:T(8,128)(2,1)S(1)}, bf16[1,128,1280]{2,1,0:T(8,128)(2,1)}, u32[]{:S(2)}) copy-start(bf16[1,128,1280]{2,1,0:T(8,128)(2,1)} %get-tuple-element.9) | copy-start | bytes 983044
  91.5 1.1 %copy-start = (bf16[1,128,1280]{2,1,0:T(8,128)(2,1)S(1)}, bf16[1,128,1280]{2,1,0:T(8,128)(2,1)}, u32[]{:S(2)}) copy-start(bf16[1,128,1280]{2,1,0:T(8,128)(2,1)} %get-tuple-element.10) | copy-start | bytes 983044
  92.6 0.9 copy-start.2

commit v5 on v4

--- a/solution.py
+++ b/solution.py
@@ -42,7 +42,7 @@
     q_buf, k_buf, v_buf, g_buf, s_buf, prob, dq_acc, done, back,
     g_own, o_own, l_own, s_own, f_own, ft_own, ft_out, ft_buf, dv_buf,
     half_send, half_recv, part, x_send, x_recv, z_send, z_recv, total,
-    in_sem, send_sem, recv_sem, ret_send, ret_recv, out_sem,
+    in_sem, send_sem, recv_sem, pair_sem, ret_send, ret_recv, value_sem, out_sem,
     f_ssem, f_rsem, y_ssem, y_rsem, d_ssem, d_rsem, x_ssem, x_rsem, z_ssem, z_rsem,
     *, scale, rows
 ):
@@ -116,6 +116,9 @@
     def target(t, block):
         return bufs[t].at[block] if t < 4 else s_buf.at[block]
 
+    def landed(t, b):
+        return pair_sem.at[0 if t == 0 else 1, b] if t in (0, 3) else recv_sem.at[t]
+
     def send_all(kinds):
         def send(i, _):
             head = head_at(i)
@@ -126,14 +129,14 @@
                 for t in kinds:
                     pltpu.make_async_remote_copy(
                         src_ref=source(t, head), dst_ref=target(t, me),
-                        send_sem=send_sem.at[t, head], recv_sem=recv_sem.at[t, me],
+                        send_sem=send_sem.at[t], recv_sem=landed(t, z),
                         device_id={"x_lo": ox, "z": oz}, device_id_type=MESH).start()
 
             @pl.when(head == mine)
             def _():
                 for t in kinds:
                     if t < 4:
-                        pltpu.make_async_copy(source(t, head), target(t, me), recv_sem.at[t, me]).start()
+                        pltpu.make_async_copy(source(t, head), target(t, me), landed(t, z)).start()
                     else:
                         s_buf[me] = s_own[head]
 
@@ -189,15 +192,16 @@
             feature_copy(w, j).start()
         ft_buf[w, :, my_span(w)] = ft_out[w, near[w]]
 
+    def gone(ref, sem):
+        pltpu.make_async_copy(ref, ref, sem).wait()
+
     def left(kinds):
-        def one(head, _):
-            @pl.when(head != mine)
-            def _():
-                for t in kinds:
-                    pltpu.make_async_copy(source(t, head), target(t, me), send_sem.at[t, head]).wait()
-            return 0
-
-        lax.fori_loop(0, HEADS, one, 0)
+        def count(n):
+            for t in kinds:
+                gone(ins[t].at[0, :, : n * SPAN] if t < 4 else s_own.at[:n], send_sem.at[t])
+
+        pl.when(active)(lambda: count(HEADS - 1))
+        pl.when(jnp.logical_not(active))(lambda: count(HEADS))
 
     left((1, 2))
     left((0,))
@@ -207,7 +211,7 @@
         return pltpu.make_async_remote_copy(
             src_ref=back.at[0, :, cols_of(h)],
             dst_ref=dv_buf.at[w, my_span(w), cols_of(h - HALF * w)],
-            send_sem=y_ssem.at[h, o], recv_sem=y_rsem.at[near[w], h],
+            send_sem=y_ssem.at[0], recv_sem=y_rsem.at[w, near[w]],
             device_id=near_id[w](lax.rem(near[w] + o, 4)), device_id_type=MESH)
 
     def pass_on(i, _):
@@ -215,7 +219,7 @@
 
         @pl.when(h != mine)
         def _():
-            pltpu.make_async_copy(done.at[0, 0], back.at[0, :, cols_of(h)], ret_recv.at[0, h]).wait()
+            gone(back.at[0, :, cols_of(h)], value_sem.at[h])
 
         for w in range(2):
             @pl.when(h // HALF == w)
@@ -231,16 +235,14 @@
         return lax.rem(z + N_Z - far_first(i), N_Z)
 
     def arrive_pair(t, b):
-        for xx in range(2):
-            r = 2 * b + xx
-            pltpu.make_async_copy(source(t, 0), target(t, r), recv_sem.at[t, r]).wait()
+        gone(bufs[t].at[pl.ds(2 * b, 2)], landed(t, b))
 
     def give(t, r):
         @pl.when(r != me)
         def _():
             pltpu.make_async_remote_copy(
                 src_ref=done.at[t, r], dst_ref=back.at[t, :, cols_of(mine)],
-                send_sem=ret_send.at[t, r], recv_sem=ret_recv.at[t, mine],
+                send_sem=ret_send.at[t], recv_sem=value_sem.at[mine] if t == 0 else ret_recv.at[t],
                 device_id=cp_id(r), device_id_type=MESH).start()
 
         @pl.when(r == me)
@@ -249,19 +251,9 @@
 
     @pl.when(active)
     def _():
-        def arrive(kinds):
-            def one(r, _):
-                for t in kinds:
-                    if t < 4:
-                        pltpu.make_async_copy(source(t, 0), target(t, r), recv_sem.at[t, r]).wait()
-                    else:
-                        @pl.when(r != me)
-                        def _():
-                            pltpu.make_async_copy(source(t, 0), target(t, r), recv_sem.at[t, r]).wait()
-                return 0
-            lax.fori_loop(0, N_CP, one, 0)
-
-        arrive((1, 2, 4))
+        gone(q_buf, recv_sem.at[1])
+        gone(g_buf, recv_sem.at[2])
+        gone(s_buf.at[: N_CP - 1], recv_sem.at[4])
         lse = jnp.concatenate([s_buf[i, 0:1, :] for i in range(N_CP)], axis=1)
 
         def value_step(i, _):
@@ -328,13 +320,8 @@
     outs = (dv_out, dk_out, dq_out)
 
     def collect_all(t):
-        def collect(h, _):
-            @pl.when(h != mine)
-            def _():
-                pltpu.make_async_copy(done.at[t, 0], back.at[t, :, cols_of(h)], ret_recv.at[t, h]).wait()
-            return 0
-
-        lax.fori_loop(0, HEADS, collect, 0)
+        pl.when(active)(lambda: gone(back.at[t, :, : (HEADS - 1) * SPAN], ret_recv.at[t]))
+        pl.when(jnp.logical_not(active))(lambda: gone(back.at[t], ret_recv.at[t]))
         pltpu.make_async_copy(back.at[t], outs[t].at[0], out_sem.at[t]).start()
 
     pltpu.make_async_copy(back.at[0], outs[0].at[0], out_sem.at[0]).start()
@@ -346,15 +333,9 @@
             feature_copy(w, j).wait()
 
     def values_from(w):
-        def one(i, _):
-            source_at, at = lax.rem(near[w] + 1 + i // HALF, 4), lax.rem(i, HALF)
-            rs = pl.ds(pl.multiple_of(source_at * SPAN, SPAN), SPAN)
-            pltpu.make_async_copy(
-                back.at[0, :, cols_of(at)], dv_buf.at[w, rs, cols_of(at)],
-                y_rsem.at[source_at, HALF * w + at]).wait()
-            return 0
-
-        lax.fori_loop(0, 3 * HALF, one, 0)
+        for o in range(1, 4):
+            peer = lax.rem(near[w] + o, 4)
+            gone(dv_buf.at[w, pl.ds(pl.multiple_of(peer * SPAN, SPAN), SPAN), :], y_rsem.at[w, peer])
 
     def part_of(w, which):
         rs = pl.ds(pl.multiple_of(which * 2 * blk, 2 * blk), 2 * blk)
@@ -385,8 +366,8 @@
 
     def z_copy(w, zz):
         return pltpu.make_async_remote_copy(
-            src_ref=z_send.at[w, zz], dst_ref=z_recv.at[xl, z], send_sem=z_ssem.at[w, zz],
-            recv_sem=z_rsem.at[xl, z], device_id={"x_lo": w, "z": zz}, device_id_type=MESH)
+            src_ref=z_send.at[w, zz], dst_ref=z_recv.at[xl, z], send_sem=z_ssem.at[w],
+            recv_sem=z_rsem.at[xl], device_id={"x_lo": w, "z": zz}, device_id_type=MESH)
 
     def is_here(w, zz):
         return jnp.logical_and(xl == w, zz == z)
@@ -422,56 +403,57 @@
     left((4, 3))
     @pl.when(active)
     def _():
-        def gave(j, _):
-            peer = lax.rem(me + j, N_CP)
-            for t in range(3):
-                pltpu.make_async_copy(
-                    done.at[t, peer], back.at[t, :, cols_of(mine)], ret_send.at[t, peer]).wait()
-            return 0
-
-        lax.fori_loop(1, N_CP, gave, 0)
-
-    def passed(h, _):
-        for w in range(2):
-            @pl.when(h // HALF == w)
-            def _():
-                for o in range(1, 4):
-                    value_copy(w, h, o).wait_send()
-        return 0
-
-    lax.fori_loop(0, HEADS, passed, 0)
+        for t in range(3):
+            gone(done.at[t, : N_CP - 1], ret_send.at[t])
+
+    gone(dv_buf.at[:, : 3 * SPAN], y_ssem.at[0])
     for w in range(2):
         half_copy(w).wait_send()
         for o in range(1, 4):
             across_copy(w, lax.rem(across[w] + o, 4)).wait_send()
 
-    total[...] = jnp.zeros_like(total)
+    def all_blocks(buf, side, sem):
+        pl.when(xl == side)(lambda: gone(buf.at[side, : N_Z - 1], sem.at[side]))
+        pl.when(xl != side)(lambda: gone(buf.at[side], sem.at[side]))
+
     for xs in range(2):
-        def take(i, _):
-            zz = lax.rem(z + far_first(i), N_Z)
-
-            @pl.when(jnp.logical_not(jnp.logical_and(xl == xs, zz == z)))
-            def _():
-                pltpu.make_async_copy(z_send.at[0, zz], z_recv.at[xs, zz], z_rsem.at[xs, zz]).wait()
-
-            total[xs * piece : (xs + 1) * piece] += z_recv[xs, zz][:, :col].astype(F32)
-            return 0
-
-        lax.fori_loop(0, N_Z, take, 0)
+        all_blocks(z_recv, xs, z_rsem)
+        rs = slice(xs * piece, (xs + 1) * piece)
+        total[rs] = sum(z_recv[xs, zz][:, :col].astype(F32) for zz in range(N_Z))
     last = pltpu.make_async_copy(total, dw_out, out_sem.at[3])
     last.start()
 
-    def z_sent(zz, _):
-        for w in range(2):
-            @pl.when(jnp.logical_not(is_here(w, zz)))
-            def _():
-                z_copy(w, zz).wait_send()
-        return 0
-
-    lax.fori_loop(0, N_Z, z_sent, 0)
+    for w in range(2):
+        all_blocks(z_send, w, z_ssem)
     for t in range(3):
         pltpu.make_async_copy(back.at[t], outs[t].at[0], out_sem.at[t]).wait()
     last.wait()
+
+
+def hand_over_kernel(*refs):
+    ins, outs, bufs, sems = refs[:4], refs[4:8], refs[8:12], refs[12]
+    first = [pltpu.make_async_copy(a, b, sems.at[0, i]) for i, (a, b) in enumerate(zip(ins, bufs))]
+    then = [pltpu.make_async_copy(b, a, sems.at[1, i]) for i, (a, b) in enumerate(zip(outs, bufs))]
+    for c in first:
+        c.start()
+    for c, d in zip(first, then):
+        c.wait()
+        d.start()
+    for d in then:
+        d.wait()
+
+
+def hand_over(*arrays):
+    any_spec = pl.BlockSpec(memory_space=pl.ANY)
+    return pl.pallas_call(
+        hand_over_kernel,
+        out_shape=tuple(jax.ShapeDtypeStruct(a.shape, a.dtype) for a in arrays),
+        in_specs=[any_spec] * 4,
+        out_specs=(any_spec,) * 4,
+        scratch_shapes=[pltpu.VMEM(a.shape, a.dtype) for a in arrays]
+        + [pltpu.SemaphoreType.DMA((2, 4))],
+        name="hand_over",
+    )(*arrays)
 
 
 def on_device(features, query_rows, key_rows, value_rows, attn_output, grad_output, log_sums):
@@ -483,7 +465,7 @@
     block = pltpu.VMEM((N_CP, rows, SPAN), BF16)
     out = jax.ShapeDtypeStruct(query_rows.shape, BF16)
     dma = pltpu.SemaphoreType.DMA
-    return pl.pallas_call(
+    results = pl.pallas_call(
         functools.partial(step_kernel, scale=SPAN**-0.5, rows=rows),
         out_shape=(out, out, out, jax.ShapeDtypeStruct((blk, half_w // N_Z), F32)),
         in_specs=[any_spec] * 7,
@@ -513,15 +495,16 @@
             pltpu.VMEM((2, N_Z, blk // 2, SPAN), BF16),
             pltpu.VMEM((blk, half_w // N_Z), F32),
             dma((4,)),
-            dma((5, HEADS)), dma((5, N_CP)), dma((3, N_CP)), dma((3, HEADS)), dma((4,)),
-            dma((2, 4)), dma((2, 4)), dma((HEADS, 4)), dma((4, HEADS)), dma((2,)), dma((2,)),
-            dma((2, 4)), dma((2, 4)), dma((2, N_Z)), dma((2, N_Z)),
+            dma((5,)), dma((5,)), dma((2, N_Z)), dma((3,)), dma((3,)), dma((HEADS,)), dma((4,)),
+            dma((2, 4)), dma((2, 4)), dma((1,)), dma((2, 4)), dma((2,)), dma((2,)),
+            dma((2, 4)), dma((2, 4)), dma((2,)), dma((2,)),
         ],
         compiler_params=pltpu.CompilerParams(
             collective_id=0, has_side_effects=True, vmem_limit_bytes=60 * 2**20),
         name="step",
     )(features, query_rows, key_rows, value_rows, attn_output, grad_output,
       jnp.transpose(log_sums, (2, 0, 1)))
+    return hand_over(*results)
 
 
 def solution(mesh):

time: 94.3 us -> 88.9 us (0.943)
  local copies, waits for them, and re-layouts: 4.43 us -> 0 us
  Pallas kernels: 89.1 us -> 88.1 us
    unnamed x10 -> x0, local copies, waits for them, and re-layouts: 4.43 us -> none
    pallas_call x1, Pallas kernels: 89.1 us -> 86.1 us  [on_device(): pl.pallas_call(functools.partial(step_kernel, scale=SPAN ** (-0.5), rows=...]
    pallas_call x0 -> x1, Pallas kernels: none -> 2 us  [hand_over(): pl.pallas_call(hand_over_kernel, out_shape=tuple((jax.ShapeDtypeStruct(a....]
where the time goes in v5:
time: 88.9 us; the launch traced here: 88.8 us
  Pallas kernels  88.1 us (99%)
    pallas_call x1, Pallas kernels, on_device(): pl.pallas_call(functools.partial(step_kernel, scale=SPAN ** (-0.5), rows=...  86.1 us
    pallas_call x1, Pallas kernels, hand_over(): pl.pallas_call(hand_over_kernel, out_shape=tuple((jax.ShapeDtypeStruct(a....  2 us

profile of v5, /device:TPU:19, one launch (start us, length us, event | category | flops | bytes accessed | tf_op | source)
XLA Modules:
  0.0 88.8 jit_solution(14451444510914950230)
XLA Ops:
  0.6 86.1 %step.1 = (bf16[1,128,1280]{2,1,0:T(8,128)(2,1)}, bf16[1,128,1280]{2,1,0:T(8,128)(2,1)}, bf16[1,128,1280]{2,1,0:T(8,128)(2,1)}, f32[160,80]{1,0:T(8,128)}) custom-call(bf16[1,128,2560]{2,1,0:T(8,128)(2,1)} %f_in.1, bf16[1,128,1280]{2,1,0:T(8,128)(2,1)} %q_in.1, bf16[1,128,1280]{2,1,0:T(8,128)(2,1)} %k_in.1, bf16[1,128,1280]{2,1,0:T(8,128)(2,1)} %v_in.1, ...), custom_call_target="tpu_custom_call" | custom-call | tf_op jit(solution)/shard_map/step/pallas_call | solution.py:468
  86.8 2.0 %hand_over.1 = (bf16[1,128,1280]{2,1,0:T(8,128)(2,1)}, bf16[1,128,1280]{2,1,0:T(8,128)(2,1)}, bf16[1,128,1280]{2,1,0:T(8,128)(2,1)}, f32[160,80]{1,0:T(8,128)}) custom-call(bf16[1,128,1280]{2,1,0:T(8,128)(2,1)} %get-tuple-element.8.refs_0_, bf16[1,128,1280]{2,1,0:T(8,128)(2,1)} %get-tuple-element.9.refs_1_, bf16[1,128,1280]{2,1,0:T(8,128)(2,1)} %get-tuple-element.10.refs_2_, ...), custom_call_target="tpu_custom_call" | custom-call | tf_op jit(solution)/shard_map/hand_over/pallas_call | solution.py:448

commit v6 on v5

--- a/solution.py
+++ b/solution.py
@@ -205,7 +205,6 @@
 
     left((1, 2))
     left((0,))
-    send_all((3,))
 
     def value_copy(w, h, o):
         return pltpu.make_async_remote_copy(
@@ -313,7 +312,9 @@
     def passes(lo, hi):
         lax.fori_loop(lo, hi, pass_on, 0)
 
-    passes(0, HEADS)
+    passes(0, 1)
+    send_all((3,))
+    passes(1, HEADS)
     key_steps(0, N_Z)
     pl.when(active)(finish_queries)
 
@@ -355,7 +356,6 @@
         values_from(w)
         half_send[w] = part_of(w, 1 - core).astype(BF16)
         half_copy(w).start()
-    for w in range(2):
         part[...] = part_of(w, core)
         half_copy(w).wait_recv()
         both = (part[...] + half_recv[w].astype(F32)).astype(BF16)

time: 88.9 us -> 86.1 us (0.969)
  Pallas kernels: 88.1 us -> 84.6 us
    pallas_call x1, Pallas kernels: 86.1 us -> 82.6 us  [on_device(): pl.pallas_call(functools.partial(step_kernel, scale=SPAN ** (-0.5), rows=...]
where the time goes in v6:
time: 86.1 us; the launch traced here: 85.2 us
  Pallas kernels  84.6 us (98%)
    pallas_call x1, Pallas kernels, on_device(): pl.pallas_call(functools.partial(step_kernel, scale=SPAN ** (-0.5), rows=...  82.6 us
    pallas_call x1, Pallas kernels, hand_over(): pl.pallas_call(hand_over_kernel, out_shape=tuple((jax.ShapeDtypeStruct(a....  2 us

profile of v6, /device:TPU:19, one launch (start us, length us, event | category | flops | bytes accessed | tf_op | source)
XLA Modules:
  0.0 85.2 jit_solution(11787042563642842500)
XLA Ops:
  0.6 82.6 %step.1 = (bf16[1,128,1280]{2,1,0:T(8,128)(2,1)}, bf16[1,128,1280]{2,1,0:T(8,128)(2,1)}, bf16[1,128,1280]{2,1,0:T(8,128)(2,1)}, f32[160,80]{1,0:T(8,128)}) custom-call(bf16[1,128,2560]{2,1,0:T(8,128)(2,1)} %f_in.1, bf16[1,128,1280]{2,1,0:T(8,128)(2,1)} %q_in.1, bf16[1,128,1280]{2,1,0:T(8,128)(2,1)} %k_in.1, bf16[1,128,1280]{2,1,0:T(8,128)(2,1)} %v_in.1, ...), custom_call_target="tpu_custom_call" | custom-call | tf_op jit(solution)/shard_map/step/pallas_call | solution.py:468
  83.2 2.0 %hand_over.1 = (bf16[1,128,1280]{2,1,0:T(8,128)(2,1)}, bf16[1,128,1280]{2,1,0:T(8,128)(2,1)}, bf16[1,128,1280]{2,1,0:T(8,128)(2,1)}, f32[160,80]{1,0:T(8,128)}) custom-call(bf16[1,128,1280]{2,1,0:T(8,128)(2,1)} %get-tuple-element.8.refs_0_, bf16[1,128,1280]{2,1,0:T(8,128)(2,1)} %get-tuple-element.9.refs_1_, bf16[1,128,1280]{2,1,0:T(8,128)(2,1)} %get-tuple-element.10.refs_2_, ...), custom_call_target="tpu_custom_call" | custom-call | tf_op jit(solution)/shard_map/hand_over/pallas_call | solution.py:448

commit v7 on v6

--- a/solution.py
+++ b/solution.py
@@ -188,8 +188,9 @@
             device_id_type=MESH)
 
     for w in range(2):
-        for j in range(1, 4):
-            feature_copy(w, j).start()
+        if w == 0:
+            for j in range(1, 4):
+                feature_copy(w, j).start()
         ft_buf[w, :, my_span(w)] = ft_out[w, near[w]]
 
     def gone(ref, sem):
@@ -204,6 +205,8 @@
         pl.when(jnp.logical_not(active))(lambda: count(HEADS))
 
     left((1, 2))
+    for j in range(1, 4):
+        feature_copy(1, j).start()
     left((0,))
 
     def value_copy(w, h, o):
@@ -285,7 +288,7 @@
         ds = (p * (dp - delta)).astype(BF16)
         dk = jnp.dot(ds, q_buf[...].reshape(seq, SPAN), preferred_element_type=F32)
         done[1, us] = (dk * scale).astype(BF16).reshape(UB, rows, SPAN)
-        dq_acc[...] += lax.dot_general(ds, k, TN, preferred_element_type=F32)
+        dq_acc[...] += lax.dot_general(k, ds, TN, preferred_element_type=F32)
         give(1, 2 * b)
         give(1, 2 * b + 1)
 
@@ -299,7 +302,7 @@
         lax.fori_loop(lo, hi, one, 0)
 
     def finish_queries():
-        done[2] = (dq_acc[...] * scale).astype(BF16).reshape(N_CP, rows, SPAN)
+        done[2] = (dq_acc[...].T * scale).astype(BF16).reshape(N_CP, rows, SPAN)
 
         def query_give(i, _):
             b = block_at(i)
@@ -312,9 +315,8 @@
     def passes(lo, hi):
         lax.fori_loop(lo, hi, pass_on, 0)
 
-    passes(0, 1)
     send_all((3,))
-    passes(1, HEADS)
+    passes(0, HEADS)
     key_steps(0, N_Z)
     pl.when(active)(finish_queries)
 
@@ -474,7 +476,7 @@
             block, block, block, block,
             pltpu.VMEM((N_CP, 8, rows), F32),
             pltpu.VMEM((seq, seq), F32),
-            pltpu.VMEM((seq, SPAN), F32),
+            pltpu.VMEM((SPAN, seq), F32),
             pltpu.VMEM((3, N_CP, rows, SPAN), BF16),
             pltpu.VMEM((3, rows, width), BF16),
             pltpu.VMEM((rows, width), BF16),

time: 86.1 us -> 84.9 us (0.986)
  Pallas kernels: 84.6 us -> 83.5 us
    pallas_call x1, Pallas kernels: 82.6 us -> 81.5 us  [on_device(): pl.pallas_call(functools.partial(step_kernel, scale=SPAN ** (-0.5), rows=...]
where the time goes in v7:
time: 84.9 us; the launch traced here: 84.1 us
  Pallas kernels  83.5 us (98%)
    pallas_call x1, Pallas kernels, on_device(): pl.pallas_call(functools.partial(step_kernel, scale=SPAN ** (-0.5), rows=...  81.5 us
    pallas_call x1, Pallas kernels, hand_over(): pl.pallas_call(hand_over_kernel, out_shape=tuple((jax.ShapeDtypeStruct(a....  2 us

profile of v7, /device:TPU:19, one launch (start us, length us, event | category | flops | bytes accessed | tf_op | source)
XLA Modules:
  0.0 84.1 jit_solution(9256825804351346536)
XLA Ops:
  0.6 81.5 %step.1 = (bf16[1,128,1280]{2,1,0:T(8,128)(2,1)}, bf16[1,128,1280]{2,1,0:T(8,128)(2,1)}, bf16[1,128,1280]{2,1,0:T(8,128)(2,1)}, f32[160,80]{1,0:T(8,128)}) custom-call(bf16[1,128,2560]{2,1,0:T(8,128)(2,1)} %f_in.1, bf16[1,128,1280]{2,1,0:T(8,128)(2,1)} %q_in.1, bf16[1,128,1280]{2,1,0:T(8,128)(2,1)} %k_in.1, bf16[1,128,1280]{2,1,0:T(8,128)(2,1)} %v_in.1, ...), custom_call_target="tpu_custom_call" | custom-call | tf_op jit(solution)/shard_map/step/pallas_call | solution.py:470
  82.1 2.0 %hand_over.1 = (bf16[1,128,1280]{2,1,0:T(8,128)(2,1)}, bf16[1,128,1280]{2,1,0:T(8,128)(2,1)}, bf16[1,128,1280]{2,1,0:T(8,128)(2,1)}, f32[160,80]{1,0:T(8,128)}) custom-call(bf16[1,128,1280]{2,1,0:T(8,128)(2,1)} %get-tuple-element.8.refs_0_, bf16[1,128,1280]{2,1,0:T(8,128)(2,1)} %get-tuple-element.9.refs_1_, bf16[1,128,1280]{2,1,0:T(8,128)(2,1)} %get-tuple-element.10.refs_2_, ...), custom_call_target="tpu_custom_call" | custom-call | tf_op jit(solution)/shard_map/hand_over/pallas_call | solution.py:450

commit v8 on v7

--- a/solution.py
+++ b/solution.py
@@ -302,10 +302,11 @@
         lax.fori_loop(lo, hi, one, 0)
 
     def finish_queries():
-        done[2] = (dq_acc[...].T * scale).astype(BF16).reshape(N_CP, rows, SPAN)
-
         def query_give(i, _):
             b = block_at(i)
+            cs = pl.ds(pl.multiple_of(b * UB * rows, UB * rows), UB * rows)
+            turned = (dq_acc[:, cs].T * scale).astype(BF16)
+            done[2, pl.ds(b * UB, UB)] = turned.reshape(UB, rows, SPAN)
             give(2, 2 * b)
             give(2, 2 * b + 1)
             return 0

time: 84.9 us -> 85.3 us (level)
  no operation moved by 1% of the time
where the time goes in v8:
time: 85.3 us; the launch traced here: 84.3 us
  Pallas kernels  83.6 us (98%)
    pallas_call x1, Pallas kernels, on_device(): pl.pallas_call(functools.partial(step_kernel, scale=SPAN ** (-0.5), rows=...  81.6 us
    pallas_call x1, Pallas kernels, hand_over(): pl.pallas_call(hand_over_kernel, out_shape=tuple((jax.ShapeDtypeStruct(a....  2 us

profile of v8, /device:TPU:19, one launch (start us, length us, event | category | flops | bytes accessed | tf_op | source)
XLA Modules:
  0.0 84.3 jit_solution(4096804287338122661)
XLA Ops:
  0.6 81.6 %step.1 = (bf16[1,128,1280]{2,1,0:T(8,128)(2,1)}, bf16[1,128,1280]{2,1,0:T(8,128)(2,1)}, bf16[1,128,1280]{2,1,0:T(8,128)(2,1)}, f32[160,80]{1,0:T(8,128)}) custom-call(bf16[1,128,2560]{2,1,0:T(8,128)(2,1)} %f_in.1, bf16[1,128,1280]{2,1,0:T(8,128)(2,1)} %q_in.1, bf16[1,128,1280]{2,1,0:T(8,128)(2,1)} %k_in.1, bf16[1,128,1280]{2,1,0:T(8,128)(2,1)} %v_in.1, ...), custom_call_target="tpu_custom_call" | custom-call | tf_op jit(solution)/shard_map/step/pallas_call | solution.py:471
  82.3 2.0 %hand_over.1 = (bf16[1,128,1280]{2,1,0:T(8,128)(2,1)}, bf16[1,128,1280]{2,1,0:T(8,128)(2,1)}, bf16[1,128,1280]{2,1,0:T(8,128)(2,1)}, f32[160,80]{1,0:T(8,128)}) custom-call(bf16[1,128,1280]{2,1,0:T(8,128)(2,1)} %get-tuple-element.8.refs_0_, bf16[1,128,1280]{2,1,0:T(8,128)(2,1)} %get-tuple-element.9.refs_1_, bf16[1,128,1280]{2,1,0:T(8,128)(2,1)} %get-tuple-element.10.refs_2_, ...), custom_call_target="tpu_custom_call" | custom-call | tf_op jit(solution)/shard_map/hand_over/pallas_call | solution.py:451
